TPU v7x, 16 devices: a whole 2x2x2 slice. The times are simulated.
16 devices in a mesh: dz: 2 (over z), dy: 2 (over y), dx: 4 (over x, core).
Axes of the slice: x: 2, y: 2, z: 2, core: 2. Of those that a mesh axis runs over, the one named last changes fastest.
Arguments:
- x_one: bfloat16 [32768, 1024], P(('dz', 'dy', 'dx'))
- g_one: bfloat16 [32768, 1024], P(('dz', 'dy', 'dx'))
- x_two: bfloat16 [32768, 1024], P(('dz', 'dy', 'dx'))
- g_two: bfloat16 [32768, 1024], P(('dz', 'dy', 'dx'))
- w_one: bfloat16 [1024, 2816], replicated
- w_two: bfloat16 [2816, 1024], replicated
- w_three: bfloat16 [1024, 2816], replicated
- w_four: bfloat16 [2816, 1024], replicated
Outputs:
- output 1: float32 [1024, 2816], replicated
- output 2: float32 [2816, 1024], replicated
- output 3: float32 [1024, 2816], replicated
- output 4: float32 [2816, 1024], replicated
- output 5: bfloat16 [32768, 1024], P(('dz', 'dy', 'dx'))
- output 6: bfloat16 [32768, 1024], P(('dz', 'dy', 'dx'))
All inputs are finite; a program needn't handle non-finite values.
Results may differ from a plain program's by a relative error of at most 0.00348054.
Values are sent between devices in bfloat16 or wider.
A program may use at most 1 GiB of HBM per device.

v0:
```python
import jax
import jax.numpy as jnp
from jax import lax
from jax.sharding import PartitionSpec as P

GELU_C = 0.7978845608028654
GELU_A = 0.044715


def gelu_value(pre_act):
    pre_f = pre_act.astype(jnp.float32)
    return 0.5 * pre_f * (1.0 + jnp.tanh(GELU_C * (pre_f + GELU_A * pre_f * pre_f * pre_f)))


def gelu_slope(pre_act):
    pre_f = pre_act.astype(jnp.float32)
    tanh_val = jnp.tanh(GELU_C * (pre_f + GELU_A * pre_f * pre_f * pre_f))
    return 0.5 * (1.0 + tanh_val) + 0.5 * pre_f * (1.0 - tanh_val * tanh_val) * GELU_C * (1.0 + 3.0 * GELU_A * pre_f * pre_f)


def mat_tn(left_op, right_op):
    return lax.dot_general(left_op, right_op, (((0,), (0,)), ((), ())), preferred_element_type=jnp.float32)


def mat_nt(left_op, right_op):
    return lax.dot_general(left_op, right_op, (((1,), (1,)), ((), ())), preferred_element_type=jnp.float32)


def local_grads(x_rows, g_rows, w_one, w_two, w_three, w_four):
    pre_one = jnp.dot(x_rows, w_one, preferred_element_type=jnp.float32).astype(jnp.bfloat16)
    act_one = gelu_value(pre_one).astype(jnp.bfloat16)
    act_two = (jnp.dot(act_one, w_two, preferred_element_type=jnp.float32) + x_rows.astype(jnp.float32)).astype(jnp.bfloat16)
    pre_three = jnp.dot(act_two, w_three, preferred_element_type=jnp.float32).astype(jnp.bfloat16)
    act_three = gelu_value(pre_three).astype(jnp.bfloat16)
    grad_four = mat_tn(act_three, g_rows)
    dz_three = (mat_nt(g_rows, w_four) * gelu_slope(pre_three)).astype(jnp.bfloat16)
    grad_three = mat_tn(act_two, dz_three)
    dh_two = (mat_nt(dz_three, w_three) + g_rows.astype(jnp.float32)).astype(jnp.bfloat16)
    grad_two = mat_tn(act_one, dh_two)
    dz_one = (mat_nt(dh_two, w_two) * gelu_slope(pre_one)).astype(jnp.bfloat16)
    grad_one = mat_tn(x_rows, dz_one)
    dx_rows = (mat_nt(dz_one, w_one) + dh_two.astype(jnp.float32)).astype(jnp.bfloat16)
    return (grad_one, grad_two, grad_three, grad_four), dx_rows


def solution(mesh):
    dev_count = mesh.shape["dz"] * mesh.shape["dy"] * mesh.shape["dx"]
    row_spec = P(("dz", "dy", "dx"), None)
    rep_spec = P(None, None)

    def mean_over_devices(grad_sum):
        shard_sum = lax.psum_scatter(grad_sum, "dx", scatter_dimension=0, tiled=True)
        shard_sum = lax.psum_scatter(shard_sum, "dy", scatter_dimension=0, tiled=True)
        shard_sum = lax.psum_scatter(shard_sum, "dz", scatter_dimension=0, tiled=True)
        shard_mean = shard_sum / dev_count
        gathered = lax.all_gather(shard_mean, "dz", axis=0, tiled=True)
        gathered = lax.all_gather(gathered, "dy", axis=0, tiled=True)
        return lax.all_gather(gathered, "dx", axis=0, tiled=True)

    def per_device(x_one, g_one, x_two, g_two, w_one, w_two, w_three, w_four):
        grads_first, dx_first = local_grads(x_one, g_one, w_one, w_two, w_three, w_four)
        grads_second, dx_second = local_grads(x_two, g_two, w_one, w_two, w_three, w_four)
        mean_grads = [mean_over_devices(grad_a + grad_b) for grad_a, grad_b in zip(grads_first, grads_second)]
        return mean_grads[0], mean_grads[1], mean_grads[2], mean_grads[3], dx_first, dx_second

    return jax.shard_map(
        per_device,
        mesh=mesh,
        in_specs=(row_spec, row_spec, row_spec, row_spec, rep_spec, rep_spec, rep_spec, rep_spec),
        out_specs=(rep_spec, rep_spec, rep_spec, rep_spec, row_spec, row_spec),
        check_vma=False,
    )
```

profile of v0, /device:TPU:0, one launch (start us, length us, event | category | flops | bytes accessed | tf_op | source)
XLA Modules:
  0.0 1453.3 jit_solution(13571963708740806376)
XLA Ops:
  7.2 18.2 %convolution_convert_fusion.3 = bf16[2048,2816]{1,0:T(8,128)(2,1)} fusion(bf16[2048,1024]{1,0:T(8,128)(2,1)} %param.8, bf16[1024,2816]{1,0:T(8,128)(2,1)} %param.12), kind=kOutput, calls=%fused_computation.78 | convolution fusion | flops 11816927232 | bytes 21495808 | tf_op jit(solution)/shard_map/dot_general | solution.py:30
  25.5 17.5 %convolution_convert_fusion.1 = bf16[2048,2816]{1,0:T(8,128)(2,1)} fusion(bf16[2048,1024]{1,0:T(8,128)(2,1)} %param.10, bf16[1024,2816]{1,0:T(8,128)(2,1)S(1)} %copy-done), kind=kOutput, calls=%fused_computation.76 | convolution fusion | flops 11816927232 | bytes 21495808 | tf_op jit(solution)/shard_map/dot_general | solution.py:30
  43.0 18.6 %add_convert_fusion.5 = bf16[2048,1024]{1,0:T(8,128)(2,1)} fusion(bf16[2048,1024]{1,0:T(8,128)(2,1)S(1)} %copy-done.2, bf16[2816,1024]{1,0:T(8,128)(2,1)S(1)} %bitcast.47, bf16[2048,2816]{1,0:T(8,128)(2,1)} %convolution_convert_fusion.3), kind=kOutput, calls=%fused_computation.84 | convolution fusion | flops 11875123200 | bytes 25690112 | tf_op jit(solution)/shard_map/dot_general | solution.py:32
  61.6 18.1 %add_convert_fusion.3 = bf16[2048,1024]{1,0:T(8,128)(2,1)S(1)} fusion(bf16[2048,1024]{1,0:T(8,128)(2,1)} %param.10, bf16[2816,1024]{1,0:T(8,128)(2,1)S(1)} %bitcast.47, bf16[2048,2816]{1,0:T(8,128)(2,1)} %convolution_convert_fusion.1), kind=kOutput, calls=%fused_computation.82 | convolution fusion | flops 11875123200 | bytes 25690112 | tf_op jit(solution)/shard_map/dot_general | solution.py:32
  79.7 14.3 convolution_convert_fusion
  94.1 17.5 %convolution_convert_fusion.2 = bf16[2048,2816]{1,0:T(8,128)(2,1)} fusion(bf16[2048,1024]{1,0:T(8,128)(2,1)} %add_convert_fusion.5, bf16[1024,2816]{1,0:T(8,128)(2,1)S(1)} %bitcast.43), kind=kOutput, calls=%fused_computation.77 | convolution fusion | flops 11816927232 | bytes 21495808 | tf_op jit(solution)/shard_map/dot_general | solution.py:33
  111.5 22.9 %fusion.44 = f32[2816,1024]{1,0:T(8,128)} fusion(bf16[2048,1024]{1,0:T(8,128)(2,1)S(1)} %copy-done.1, bf16[2048,2816]{1,0:T(8,128)(2,1)} %convolution_convert_fusion.2), kind=kOutput, calls=%fused_computation.73 | convolution fusion | flops 11868831744 | bytes 27262976 | tf_op jit(solution)/shard_map/dot_general | solution.py:22
  134.4 24.6 %fusion.48 = f32[2816,1024]{1,0:T(8,128)} fusion(f32[2816,1024]{1,0:T(8,128)} %fusion.44, bf16[2048,1024]{1,0:T(8,128)(2,1)S(1)} %copy-done.3, bf16[2048,2816]{1,0:T(8,128)(2,1)} %convolution_convert_fusion), kind=kOutput, calls=%fused_computation.85 | convolution fusion | flops 11871715328 | bytes 38797312 | tf_op jit(solution)/shard_map/dot_general | solution.py:22
  159.1 30.6 %fusion.24 = bf16[2048,2816]{1,0:T(8,128)(2,1)} fusion(bf16[2048,2816]{1,0:T(8,128)(2,1)} %convolution_convert_fusion.2, bf16[2048,1024]{1,0:T(8,128)(2,1)} %param.9, bf16[2816,1024]{1,0:T(8,128)(2,1)} %param.15), kind=kOutput, calls=%fused_computation.52 | convolution fusion | flops 11926503424 | bytes 33030144 | tf_op jit(solution)/shard_map/dot_general | solution.py:26
  189.7 17.9 %fusion.65 = f32[1024,2816]{1,0:T(8,128)} fusion(bf16[2048,1024]{1,0:T(8,128)(2,1)S(1)} %copy-done.8, bf16[2048,2816]{1,0:T(8,128)(2,1)} %fusion.24), kind=kOutput, calls=%fused_computation.102 | convolution fusion | flops 11811160064 | bytes 27262976 | tf_op jit(solution)/shard_map/dot_general | solution.py:22
  207.6 29.0 %fusion.12 = bf16[2048,2816]{1,0:T(8,128)(2,1)} fusion(bf16[2048,2816]{1,0:T(8,128)(2,1)} %convolution_convert_fusion, bf16[2048,1024]{1,0:T(8,128)(2,1)S(1)} %copy-done.4, bf16[2816,1024]{1,0:T(8,128)(2,1)} %param.15), kind=kOutput, calls=%fused_computation.40 | convolution fusion | flops 11926503424 | bytes 33030144 | tf_op jit(solution)/shard_map/dot_general | solution.py:26
  236.6 19.7 %convolution_add_fusion.1 = f32[1024,2816]{1,0:T(8,128)} fusion(f32[1024,2816]{1,0:T(8,128)} %fusion.65, bf16[2048,1024]{1,0:T(8,128)(2,1)S(1)} %copy-done.7, bf16[2048,2816]{1,0:T(8,128)(2,1)} %fusion.12), kind=kOutput, calls=%fused_computation.87 | convolution fusion | flops 11814043648 | bytes 38797312 | tf_op jit(solution)/shard_map/dot_general | solution.py:22
  256.4 18.4 %add_convert_fusion.4 = bf16[2048,1024]{1,0:T(8,128)(2,1)S(1)} fusion(bf16[2048,1024]{1,0:T(8,128)(2,1)} %param.9, bf16[2048,2816]{1,0:T(8,128)(2,1)} %fusion.24, bf16[1024,2816]{1,0:T(8,128)(2,1)} %param.14), kind=kOutput, calls=%fused_computation.83 | convolution fusion | flops 11817451520 | bytes 25690112 | tf_op jit(solution)/shard_map/dot_general | solution.py:26
  276.9 28.8 %fusion.31 = bf16[2048,2816]{1,0:T(8,128)(2,1)} fusion(bf16[2048,2816]{1,0:T(8,128)(2,1)} %convolution_convert_fusion.3, bf16[2048,1024]{1,0:T(8,128)(2,1)S(1)} %add_convert_fusion.4, bf16[2816,1024]{1,0:T(8,128)(2,1)} %param.13), kind=kOutput, calls=%fused_computation.59 | convolution fusion | flops 11926503424 | bytes 33030144 | tf_op jit(solution)/shard_map/dot_general | solution.py:26
  305.7 19.2 %fusion.64 = f32[2816,1024]{1,0:T(8,128)} fusion(bf16[2048,2816]{1,0:T(8,128)(2,1)} %fusion.31, bf16[2048,1024]{1,0:T(8,128)(2,1)} %param.8), kind=kOutput, calls=%fused_computation.101 | convolution fusion | flops 11811160064 | bytes 27262976 | tf_op jit(solution)/shard_map/dot_general | solution.py:22
  324.9 17.0 %add_convert_fusion.2 = bf16[2048,1024]{1,0:T(8,128)(2,1)} fusion(bf16[2048,1024]{1,0:T(8,128)(2,1)} %param.11, bf16[2048,2816]{1,0:T(8,128)(2,1)} %fusion.12, bf16[1024,2816]{1,0:T(8,128)(2,1)S(1)} %bitcast.45), kind=kOutput, calls=%fused_computation.81 | convolution fusion | flops 11817451520 | bytes 25690112 | tf_op jit(solution)/shard_map/dot_general | solution.py:26
  341.9 28.9 %fusion.19 = bf16[2048,2816]{1,0:T(8,128)(2,1)} fusion(bf16[2048,2816]{1,0:T(8,128)(2,1)} %convolution_convert_fusion.1, bf16[2048,1024]{1,0:T(8,128)(2,1)} %add_convert_fusion.2, bf16[2816,1024]{1,0:T(8,128)(2,1)S(1)} %bitcast.49), kind=kOutput, calls=%fused_computation.47 | convolution fusion | flops 11926503424 | bytes 33030144 | tf_op jit(solution)/shard_map/dot_general | solution.py:26
  370.8 19.5 %add_bitcast_fusion = f32[1024,2816]{0,1:T(8,128)} fusion(f32[2816,1024]{1,0:T(8,128)} %fusion.64, bf16[2048,2816]{1,0:T(8,128)(2,1)} %fusion.19, bf16[2048,1024]{1,0:T(8,128)(2,1)S(1)} %copy-done.5), kind=kOutput, calls=%fused_computation.72 | convolution fusion | flops 11814043648 | bytes 38797312 | tf_op jit(solution)/shard_map/dot_general | solution.py:22
  390.3 23.9 %fusion.61 = f32[2816,1024]{1,0:T(8,128)} fusion(bf16[2048,1024]{1,0:T(8,128)(2,1)} %copy-done.9, bf16[2048,2816]{1,0:T(8,128)(2,1)} %convolution_convert_fusion.3), kind=kOutput, calls=%fused_computation.100 | convolution fusion | flops 11868831744 | bytes 27262976 | tf_op jit(solution)/shard_map/dot_general | solution.py:22
  414.2 24.7 %convolution_add_fusion = f32[2816,1024]{1,0:T(8,128)} fusion(f32[2816,1024]{1,0:T(8,128)} %fusion.61, bf16[2048,1024]{1,0:T(8,128)(2,1)S(1)} %copy-done.11, bf16[2048,2816]{1,0:T(8,128)(2,1)} %convolution_convert_fusion.1), kind=kOutput, calls=%fused_computation.86 | convolution fusion | flops 11871715328 | bytes 38797312 | tf_op jit(solution)/shard_map/dot_general | solution.py:22
  440.2 39.1 %reduce-scatter.17.cloned.1.call-done = f32[256,2816]{0,1:T(8,128)} async-done(((f32[1024,2816]{0,1:T(8,128)}), f32[256,2816]{0,1:T(8,128)}) %reduce-scatter.17.cloned.1.call-update) | async-done | bytes 2883600 | tf_op jit(solution)/shard_map/reduce_scatter | solution.py:52
  479.4 89.0 %reduce-scatter.21.cloned.1.call-done = f32[704,1024]{1,0:T(8,128)} async-done(((f32[2816,1024]{1,0:T(8,128)}), f32[704,1024]{1,0:T(8,128)}) %reduce-scatter.21.cloned.1.call-update) | async-done | bytes 2883600 | tf_op jit(solution)/shard_map/reduce_scatter | solution.py:52
  568.5 40.6 %reduce-scatter.33.cloned.1.call-done = f32[352,1024]{1,0:T(8,128)} async-done(((f32[704,1024]{1,0:T(8,128)}), f32[352,1024]{1,0:T(8,128)}) %reduce-scatter.33.cloned.1.call-update) | async-done | bytes 1441808 | tf_op jit(solution)/shard_map/reduce_scatter | solution.py:53
  609.1 40.6 %reduce-scatter.29.cloned.1.call-done = f32[128,2816]{1,0:T(8,128)} async-done(((f32[256,2816]{1,0:T(8,128)}), f32[128,2816]{1,0:T(8,128)}) %reduce-scatter.29.cloned.1.call-update) | async-done | bytes 1441808 | tf_op jit(solution)/shard_map/reduce_scatter | solution.py:53
  649.8 40.8 %reduce-scatter.19.cloned.1.call-done = f32[128,2816]{0,1:T(8,128)} async-done(((f32[256,2816]{0,1:T(8,128)}), f32[128,2816]{0,1:T(8,128)}) %reduce-scatter.19.cloned.1.call-update) | async-done | bytes 1441808 | tf_op jit(solution)/shard_map/reduce_scatter | solution.py:53
  693.6 37.9 %reduce-scatter.23.cloned.1.call-done = f32[352,1024]{1,0:T(8,128)} async-done(((f32[704,1024]{1,0:T(8,128)}), f32[352,1024]{1,0:T(8,128)}) %reduce-scatter.23.cloned.1.call-update) | async-done | bytes 1441808 | tf_op jit(solution)/shard_map/reduce_scatter | solution.py:53
  731.5 24.9 %reduce-scatter.35.cloned.1.call-done = f32[176,1024]{1,0:T(8,128)} async-done(((f32[352,1024]{1,0:T(8,128)}), f32[176,1024]{1,0:T(8,128)}) %reduce-scatter.35.cloned.1.call-update) | async-done | bytes 720912 | tf_op jit(solution)/shard_map/reduce_scatter | solution.py:54
  758.6 22.7 %reduce-scatter.39.cloned.1.call-done = f32[64,2816]{1,0:T(8,128)} async-done(((f32[128,2816]{1,0:T(8,128)}), f32[64,2816]{1,0:T(8,128)}) %reduce-scatter.39.cloned.1.call-update) | async-done | bytes 720912 | tf_op jit(solution)/shard_map/reduce_scatter | solution.py:54
  783.3 23.5 %reduce-scatter.37.cloned.1.call-done = f32[64,2816]{1,0:T(8,128)} async-done(((f32[128,2816]{1,0:T(8,128)}), f32[64,2816]{1,0:T(8,128)}) %reduce-scatter.37.cloned.1.call-update) | async-done | bytes 720912 | tf_op jit(solution)/shard_map/reduce_scatter | solution.py:54
  808.9 22.8 %reduce-scatter.25.cloned.1.call-done = f32[176,1024]{1,0:T(8,128)} async-done(((f32[352,1024]{1,0:T(8,128)}), f32[176,1024]{1,0:T(8,128)}) %reduce-scatter.25.cloned.1.call-update) | async-done | bytes 720912 | tf_op jit(solution)/shard_map/reduce_scatter | solution.py:54
  833.8 23.0 %all-gather.31.cloned.1.call-done = f32[352,1024]{1,0:T(8,128)} async-done(((f32[176,1024]{1,0:T(8,128)}), f32[352,1024]{1,0:T(8,128)}) %all-gather.31.cloned.1.call-update) | async-done | bytes 1441808 | tf_op jit(solution)/shard_map/all_gather | solution.py:56
  856.9 25.4 %all-gather.25.cloned.1.call-done = f32[128,2816]{1,0:T(8,128)} async-done(((f32[64,2816]{1,0:T(8,128)}), f32[128,2816]{1,0:T(8,128)}) %all-gather.25.cloned.1.call-update) | async-done | bytes 1441808 | tf_op jit(solution)/shard_map/all_gather | solution.py:56
  882.4 25.4 %all-gather.13.cloned.1.call-done = f32[128,2816]{1,0:T(8,128)} async-done(((f32[64,2816]{1,0:T(8,128)}), f32[128,2816]{1,0:T(8,128)}) %all-gather.13.cloned.1.call-update) | async-done | bytes 1441808 | tf_op jit(solution)/shard_map/all_gather | solution.py:56
  907.9 25.4 %all-gather.19.cloned.1.call-done = f32[352,1024]{1,0:T(8,128)} async-done(((f32[176,1024]{1,0:T(8,128)}), f32[352,1024]{1,0:T(8,128)}) %all-gather.19.cloned.1.call-update) | async-done | bytes 1441808 | tf_op jit(solution)/shard_map/all_gather | solution.py:56
  933.4 41.4 %all-gather.33.cloned.1.call-done = f32[704,1024]{1,0:T(8,128)} async-done(((f32[352,1024]{1,0:T(8,128)}), f32[704,1024]{1,0:T(8,128)}) %all-gather.33.cloned.1.call-update) | async-done | bytes 2883600 | tf_op jit(solution)/shard_map/all_gather | solution.py:57
  974.9 41.4 %all-gather.27.cloned.1.call-done = f32[256,2816]{1,0:T(8,128)} async-done(((f32[128,2816]{1,0:T(8,128)}), f32[256,2816]{1,0:T(8,128)}) %all-gather.27.cloned.1.call-update) | async-done | bytes 2883600 | tf_op jit(solution)/shard_map/all_gather | solution.py:57
  1016.3 41.5 %all-gather.15.cloned.1.call-done = f32[256,2816]{1,0:T(8,128)} async-done(((f32[128,2816]{1,0:T(8,128)}), f32[256,2816]{1,0:T(8,128)}) %all-gather.15.cloned.1.call-update) | async-done | bytes 2883600 | tf_op jit(solution)/shard_map/all_gather | solution.py:57
  1058.0 41.4 %all-gather.21.cloned.1.call-done = f32[704,1024]{1,0:T(8,128)} async-done(((f32[352,1024]{1,0:T(8,128)}), f32[704,1024]{1,0:T(8,128)}) %all-gather.21.cloned.1.call-update) | async-done | bytes 2883600 | tf_op jit(solution)/shard_map/all_gather | solution.py:57
  1099.4 20.9 %add_convert_fusion = bf16[2048,1024]{1,0:T(8,128)(2,1)} fusion(bf16[2048,1024]{1,0:T(8,128)(2,1)} %add_convert_fusion.2, bf16[2048,2816]{1,0:T(8,128)(2,1)} %fusion.19, bf16[1024,2816]{1,0:T(8,128)(2,1)} %param.12), kind=kOutput, calls=%fused_computation.79 | convolution fusion | flops 11817451520 | bytes 25690112 | tf_op jit(solution)/shard_map/dot_general | solution.py:26
  1120.3 15.8 %add_convert_fusion.1 = bf16[2048,1024]{1,0:T(8,128)(2,1)} fusion(bf16[2048,1024]{1,0:T(8,128)(2,1)S(1)} %copy-done.10, bf16[2048,2816]{1,0:T(8,128)(2,1)} %fusion.31, bf16[1024,2816]{1,0:T(8,128)(2,1)S(1)} %bitcast.51), kind=kOutput, calls=%fused_computation.80 | convolution fusion | flops 11817451520 | bytes 25690112 | tf_op jit(solution)/shard_map/dot_general | solution.py:26
  1136.1 39.6 %all-gather.35.cloned.1.call-done = f32[2816,1024]{1,0:T(8,128)} async-done(((f32[704,1024]{1,0:T(8,128)}), f32[2816,1024]{1,0:T(8,128)}) %all-gather.35.cloned.1.call-update) | async-done | bytes 11534352 | tf_op jit(solution)/shard_map/all_gather | solution.py:58
  1175.7 76.4 %all-gather.29.cloned.1.call-done = f32[1024,2816]{1,0:T(8,128)} async-done(((f32[256,2816]{1,0:T(8,128)}), f32[1024,2816]{1,0:T(8,128)}) %all-gather.29.cloned.1.call-update) | async-done | bytes 11534352 | tf_op jit(solution)/shard_map/all_gather | solution.py:58
  1252.1 76.4 %all-gather.17.cloned.1.call-done = f32[1024,2816]{1,0:T(8,128)} async-done(((f32[256,2816]{1,0:T(8,128)}), f32[1024,2816]{1,0:T(8,128)}) %all-gather.17.cloned.1.call-update) | async-done | bytes 11534352 | tf_op jit(solution)/shard_map/all_gather | solution.py:58
  1328.5 76.2 %all-gather.23.cloned.1.call-done = f32[2816,1024]{1,0:T(8,128)} async-done(((f32[704,1024]{1,0:T(8,128)}), f32[2816,1024]{1,0:T(8,128)}) %all-gather.23.cloned.1.call-update) | async-done | bytes 11534352 | tf_op jit(solution)/shard_map/all_gather | solution.py:58
  1404.7 9.4 copy.32
  1414.2 11.2 copy.33
  1425.3 9.4 copy.34
  1434.8 11.2 copy.35
  (104 shorter events, 15.5 us)
Async XLA Ops:
  7.2 431.9 %reduce-scatter.31.cloned.1.call-start = ((), (), s32[]{:S(2)}) async-start(), calls=%async_computation.28 | async-start | bytes 14417920 | tf_op jit(solution)/shard_map/reduce_scatter | solution.py:52
  7.2 18.2 %copy-start = (bf16[1024,2816]{1,0:T(8,128)(2,1)S(1)}, bf16[1024,2816]{1,0:T(8,128)(2,1)}, u32[]{:S(2)}) copy-start(bf16[1024,2816]{1,0:T(8,128)(2,1)} %param.12) | copy-start | bytes 17301508
  7.2 35.7 %slice-start.4 = ((s8[5767168]{0:T(1024)(128)(4,1)}), s8[4194304]{0:T(1024)(128)(4,1)S(1)}, s32[]{:S(2)}) async-start(s8[5767168]{0:T(1024)(128)(4,1)} %bitcast.46), calls=%async_computation.40 | async-start | bytes 8388608
  25.5 17.5 %slice-start.5 = ((s8[5767168]{0:T(1024)(128)(4,1)}), s8[1572864]{0:T(1024)(128)(4,1)S(1)}, s32[]{:S(2)}) async-start(s8[5767168]{0:T(1024)(128)(4,1)} %bitcast.46), calls=%async_computation.41 | async-start | bytes 3145728
  25.5 17.5 %copy-start.2 = (bf16[2048,1024]{1,0:T(8,128)(2,1)S(1)}, bf16[2048,1024]{1,0:T(8,128)(2,1)}, u32[]{:S(2)}) copy-start(bf16[2048,1024]{1,0:T(8,128)(2,1)} %param.8) | copy-start | bytes 12582916
  43.0 36.7 %slice-start = ((s8[5767168]{0:T(1024)(128)(4,1)}), s8[4194304]{0:T(1024)(128)(4,1)S(1)}, s32[]{:S(2)}) async-start(s8[5767168]{0:T(1024)(128)(4,1)} %bitcast.42), calls=%async_computation.36 | async-start | bytes 8388608
  61.6 18.1 %slice-start.1 = ((s8[5767168]{0:T(1024)(128)(4,1)}), s8[1572864]{0:T(1024)(128)(4,1)S(1)}, s32[]{:S(2)}) async-start(s8[5767168]{0:T(1024)(128)(4,1)} %bitcast.42), calls=%async_computation.37 | async-start | bytes 3145728
  79.7 14.3 copy-start.6
  94.1 17.5 %copy-start.1 = (bf16[2048,1024]{1,0:T(8,128)(2,1)S(1)}, bf16[2048,1024]{1,0:T(8,128)(2,1)}, u32[]{:S(2)}) copy-start(bf16[2048,1024]{1,0:T(8,128)(2,1)} %param.9) | copy-start | bytes 12582916
  111.5 22.9 %copy-start.3 = (bf16[2048,1024]{1,0:T(8,128)(2,1)S(1)}, bf16[2048,1024]{1,0:T(8,128)(2,1)}, u32[]{:S(2)}) copy-start(bf16[2048,1024]{1,0:T(8,128)(2,1)} %param.11) | copy-start | bytes 12582916
  159.0 280.6 %reduce-scatter.27.cloned.1.call-start = ((), (), s32[]{:S(2)}) async-start(), calls=%async_computation.23 | async-start | bytes 14417920 | tf_op jit(solution)/shard_map/reduce_scatter | solution.py:52
  159.1 30.6 %copy-start.8 = (bf16[2048,1024]{1,0:T(8,128)(2,1)S(1)}, bf16[2048,1024]{1,0:T(8,128)(2,1)}, u32[]{:S(2)}) copy-start(bf16[2048,1024]{1,0:T(8,128)(2,1)} %add_convert_fusion.5) | copy-start | bytes 12582916
  189.7 17.9 %copy-start.4 = (bf16[2048,1024]{1,0:T(8,128)(2,1)S(1)}, bf16[2048,1024]{1,0:T(8,128)(2,1)}, u32[]{:S(2)}) copy-start(bf16[2048,1024]{1,0:T(8,128)(2,1)} %param.11) | copy-start | bytes 12582916
  207.6 29.0 %copy-start.7 = (bf16[2048,1024]{1,0:T(8,128)(2,1)S(1)}, bf16[2048,1024]{1,0:T(8,128)(2,1)}, u32[]{:S(2)}) copy-start(bf16[2048,1024]{1,0:T(8,128)(2,1)} %copy-done.6) | copy-start | bytes 12582916
  256.4 222.9 %reduce-scatter.17.cloned.1.call-start = ((), (), s32[]{:S(2)}) async-start(), calls=%async_computation.12 | async-start | bytes 14417920 | tf_op jit(solution)/shard_map/reduce_scatter | solution.py:52
  256.4 68.4 %slice-start.2 = ((s8[5767168]{0:T(1024)(128)(4,1)}), s8[4194304]{0:T(1024)(128)(4,1)S(1)}, s32[]{:S(2)}) async-start(s8[5767168]{0:T(1024)(128)(4,1)} %bitcast.44), calls=%async_computation.38 | async-start | bytes 8388608
  274.9 2.0 copy-start.9
  276.9 48.0 %slice-start.3 = ((s8[5767168]{0:T(1024)(128)(4,1)}), s8[1572864]{0:T(1024)(128)(4,1)S(1)}, s32[]{:S(2)}) async-start(s8[5767168]{0:T(1024)(128)(4,1)} %bitcast.44), calls=%async_computation.39 | async-start | bytes 3145728
  305.7 36.2 %slice-start.6 = ((s8[5767168]{0:T(1024)(128)(4,1)}), s8[4194304]{0:T(1024)(128)(4,1)S(1)}, s32[]{:S(2)}) async-start(s8[5767168]{0:T(1024)(128)(4,1)} %bitcast.48), calls=%async_computation.42 | async-start | bytes 8388608
  324.9 17.0 %slice-start.7 = ((s8[5767168]{0:T(1024)(128)(4,1)}), s8[1572864]{0:T(1024)(128)(4,1)S(1)}, s32[]{:S(2)}) async-start(s8[5767168]{0:T(1024)(128)(4,1)} %bitcast.48), calls=%async_computation.43 | async-start | bytes 3145728
  341.9 28.9 %copy-start.5 = (bf16[2048,1024]{1,0:T(8,128)(2,1)S(1)}, bf16[2048,1024]{1,0:T(8,128)(2,1)}, u32[]{:S(2)}) copy-start(bf16[2048,1024]{1,0:T(8,128)(2,1)} %param.10) | copy-start | bytes 12582916
  390.3 178.1 %reduce-scatter.21.cloned.1.call-start = ((), (), s32[]{:S(2)}) async-start(), calls=%async_computation.17 | async-start | bytes 14417920 | tf_op jit(solution)/shard_map/reduce_scatter | solution.py:52
  390.3 23.9 %copy-start.11 = (bf16[2048,1024]{1,0:T(8,128)(2,1)S(1)}, bf16[2048,1024]{1,0:T(8,128)(2,1)}, u32[]{:S(2)}) copy-start(bf16[2048,1024]{1,0:T(8,128)(2,1)} %add_convert_fusion.2) | copy-start | bytes 12582916
  439.0 170.1 %reduce-scatter.33.cloned.1.call-start = ((), (), s32[]{:S(2)}) async-start(), calls=%async_computation.29 | async-start | bytes 4325376 | tf_op jit(solution)/shard_map/reduce_scatter | solution.py:53
  439.6 210.2 %reduce-scatter.29.cloned.1.call-start = ((), (), s32[]{:S(2)}) async-start(), calls=%async_computation.24 | async-start | bytes 4325376 | tf_op jit(solution)/shard_map/reduce_scatter | solution.py:53
  440.1 250.5 %reduce-scatter.19.cloned.1.call-start = ((), (), s32[]{:S(2)}) async-start(), calls=%async_computation.13 | async-start | bytes 4325376 | tf_op jit(solution)/shard_map/reduce_scatter | solution.py:53
  479.3 252.1 %reduce-scatter.23.cloned.1.call-start = ((), (), s32[]{:S(2)}) async-start(), calls=%async_computation.18 | async-start | bytes 4325376 | tf_op jit(solution)/shard_map/reduce_scatter | solution.py:53
  568.4 188.0 %reduce-scatter.35.cloned.1.call-start = ((), (), s32[]{:S(2)}) async-start(), calls=%async_computation.30 | async-start | bytes 2162688 | tf_op jit(solution)/shard_map/reduce_scatter | solution.py:54
  609.1 172.2 %reduce-scatter.39.cloned.1.call-start = ((), (), s32[]{:S(2)}) async-start(), calls=%async_computation.35 | async-start | bytes 2162688 | tf_op jit(solution)/shard_map/reduce_scatter | solution.py:54
  649.8 157.1 %reduce-scatter.37.cloned.1.call-start = ((), (), s32[]{:S(2)}) async-start(), calls=%async_computation.34 | async-start | bytes 2162688 | tf_op jit(solution)/shard_map/reduce_scatter | solution.py:54
  693.5 138.2 %reduce-scatter.25.cloned.1.call-start = ((), (), s32[]{:S(2)}) async-start(), calls=%async_computation.19 | async-start | bytes 2162688 | tf_op jit(solution)/shard_map/reduce_scatter | solution.py:54
  731.4 125.3 %all-gather.31.cloned.1.call-start = ((), (), s32[]{:S(2)}) async-start(), calls=%async_computation.31 | async-start | bytes 2162688 | tf_op jit(solution)/shard_map/all_gather | solution.py:56
  758.5 123.8 %all-gather.25.cloned.1.call-start = ((), (), s32[]{:S(2)}) async-start(), calls=%async_computation.25 | async-start | bytes 2162688 | tf_op jit(solution)/shard_map/all_gather | solution.py:56
  783.3 124.5 %all-gather.13.cloned.1.call-start = ((), (), s32[]{:S(2)}) async-start(), calls=%async_computation.14 | async-start | bytes 2162688 | tf_op jit(solution)/shard_map/all_gather | solution.py:56
  808.9 124.4 %all-gather.19.cloned.1.call-start = ((), (), s32[]{:S(2)}) async-start(), calls=%async_computation.20 | async-start | bytes 2162688 | tf_op jit(solution)/shard_map/all_gather | solution.py:56
  833.8 141.0 %all-gather.33.cloned.1.call-start = ((), (), s32[]{:S(2)}) async-start(), calls=%async_computation.32 | async-start | bytes 4325376 | tf_op jit(solution)/shard_map/all_gather | solution.py:57
  856.8 159.4 %all-gather.27.cloned.1.call-start = ((), (), s32[]{:S(2)}) async-start(), calls=%async_computation.26 | async-start | bytes 4325376 | tf_op jit(solution)/shard_map/all_gather | solution.py:57
  882.3 175.6 %all-gather.15.cloned.1.call-start = ((), (), s32[]{:S(2)}) async-start(), calls=%async_computation.15 | async-start | bytes 4325376 | tf_op jit(solution)/shard_map/all_gather | solution.py:57
  907.8 191.5 %all-gather.21.cloned.1.call-start = ((), (), s32[]{:S(2)}) async-start(), calls=%async_computation.21 | async-start | bytes 4325376 | tf_op jit(solution)/shard_map/all_gather | solution.py:57
  933.4 242.4 %all-gather.35.cloned.1.call-start = ((), (), s32[]{:S(2)}) async-start(), calls=%async_computation.33 | async-start | bytes 14417920 | tf_op jit(solution)/shard_map/all_gather | solution.py:58
  974.8 277.3 %all-gather.29.cloned.1.call-start = ((), (), s32[]{:S(2)}) async-start(), calls=%async_computation.27 | async-start | bytes 14417920 | tf_op jit(solution)/shard_map/all_gather | solution.py:58
  1016.3 312.2 %all-gather.17.cloned.1.call-start = ((), (), s32[]{:S(2)}) async-start(), calls=%async_computation.16 | async-start | bytes 14417920 | tf_op jit(solution)/shard_map/all_gather | solution.py:58
  1057.9 62.4 %slice-start.8 = ((s8[5767168]{0:T(1024)(128)(4,1)}), s8[1572864]{0:T(1024)(128)(4,1)S(1)}, s32[]{:S(2)}) async-start(s8[5767168]{0:T(1024)(128)(4,1)} %bitcast.50), calls=%async_computation.44 | async-start | bytes 3145728
  1057.9 346.8 %all-gather.23.cloned.1.call-start = ((), (), s32[]{:S(2)}) async-start(), calls=%async_computation.22 | async-start | bytes 14417920 | tf_op jit(solution)/shard_map/all_gather | solution.py:58
  1099.4 20.9 %slice-start.9 = ((s8[5767168]{0:T(1024)(128)(4,1)}), s8[4194304]{0:T(1024)(128)(4,1)S(1)}, s32[]{:S(2)}) async-start(s8[5767168]{0:T(1024)(128)(4,1)} %bitcast.50), calls=%async_computation.45 | async-start | bytes 8388608
  1099.4 20.9 %copy-start.10 = (bf16[2048,1024]{1,0:T(8,128)(2,1)S(1)}, bf16[2048,1024]{1,0:T(8,128)(2,1)}, u32[]{:S(2)}) copy-start(bf16[2048,1024]{1,0:T(8,128)(2,1)} %copy-done.9) | copy-start | bytes 12582916
Sparse Core Ops, SparseCore 0:
  159.2 88.8 reduce-scatter.30
  256.5 88.8 reduce-scatter.26
  390.4 88.8 reduce-scatter.16
  482.3 86.0 reduce-scatter.20
  570.5 38.5 reduce-scatter.32
  611.2 38.5 reduce-scatter.28
  652.0 38.5 reduce-scatter.18
  692.8 38.5 reduce-scatter.22
  733.7 22.7 reduce-scatter.34
  758.5 22.7 reduce-scatter.38
  784.1 22.7 reduce-scatter.36
  808.9 22.7 reduce-scatter.24
  833.2 23.5 all-gather.30
  858.7 23.5 all-gather.24
  884.2 23.5 all-gather.12
  909.8 23.5 all-gather.18
  934.7 40.0 all-gather.32
  976.2 40.0 all-gather.26
  1017.8 40.0 all-gather.14
  1059.3 40.0 all-gather.20
  1100.9 74.7 all-gather.34
  1177.3 74.7 all-gather.28
  1253.6 74.7 all-gather.16
  1329.9 74.7 all-gather.22
where the time goes:
time: 1460 us; the launch traced here: 1450 us
  waiting for transfers between devices  917 us (63%)
  matrix products  466 us (32%)
  local copies, waits for them, and re-layouts  46.3 us (3%)
  between operations  15.1 us (1%)
    all_gather x4, waiting for transfers between devices, mean_over_devices(): return lax.all_gather(gathered, 'dx', axis=0, tiled=True)  269 us
    dot_general x8, matrix products, mat_nt(): lax.dot_general(left_op, right_op, (((1,), (1,)), ((), ())), preferred_el...  189 us
    dot_general x8, matrix products, mat_tn(): lax.dot_general(left_op, right_op, (((0,), (0,)), ((), ())), preferred_el...  172 us
    all_gather x4, waiting for transfers between devices, mean_over_devices(): gathered = lax.all_gather(gathered, 'dy', axis=0, tiled=True)  166 us
    reduce_scatter x4, waiting for transfers between devices, mean_over_devices(): lax.psum_scatter(shard_sum, 'dy', scatter_dimension=0, tiled=True)  160 us
    reduce_scatter x4, waiting for transfers between devices, mean_over_devices(): lax.psum_scatter(grad_sum, 'dx', scatter_dimension=0, tiled=True)  128 us
    all_gather x4, waiting for transfers between devices, mean_over_devices(): gathered = lax.all_gather(shard_mean, 'dz', axis=0, tiled=True)  99.3 us
    reduce_scatter x4, waiting for transfers between devices, mean_over_devices(): lax.psum_scatter(shard_sum, 'dz', scatter_dimension=0, tiled=True)  93.9 us
  transfers between devices with their start and end apart: 24, of which 22 were waited for; matrix products, arithmetic and copies ran while one was open for 22% of the time, Pallas kernels for 0%

commit v1 on v0

v1 whole, which is shorter than its diff:
```python
import jax
import jax.numpy as jnp
from jax import lax
from jax.experimental import pallas as pl
from jax.experimental.pallas import tpu as pltpu
from jax.sharding import PartitionSpec as P

GELU_C = 0.7978845608028654
GELU_A = 0.044715
AXES = ("dz", "dy", "dx")
BF16 = jnp.bfloat16
F32 = jnp.float32
VMEM_LIMIT = 64000000
MESH = pl.DeviceIdType.MESH
CHUNK = 256
SLOTS = 5
CUTS_UPPER = (0, 11)
CUTS_LOWER = (0, 6, 11)
COLOUR_AXES = ((2, 1, 0), (1, 0, 2), (0, 2, 1))


def gelu_value(pre_act):
    pre_f = pre_act.astype(F32)
    return 0.5 * pre_f * (1.0 + jnp.tanh(GELU_C * (pre_f + GELU_A * pre_f * pre_f * pre_f)))


def dot_nn(lhs, rhs):
    return lax.dot_general(lhs, rhs, (((1,), (0,)), ((), ())), preferred_element_type=F32)


def dot_nt(lhs, rhs):
    return lax.dot_general(lhs, rhs, (((1,), (1,)), ((), ())), preferred_element_type=F32)


def dot_tn(lhs, rhs):
    return lax.dot_general(lhs, rhs, (((0,), (0,)), ((), ())), preferred_element_type=F32)


class Reducer:
    def __init__(self, rows, cols, by_rows, small):
        self.rows, self.cols, self.by_rows = rows, cols, by_rows
        tiles, unit = (rows // 8, 8) if by_rows else (cols // 128, 128)
        base, extra = tiles // 3, tiles % 3
        order = [(small + 1 + k) % 3 for k in range(3)]
        sizes = [0, 0, 0]
        for pos, colour in enumerate(order):
            sizes[colour] = (base + (1 if pos < extra else 0)) * unit
        self.parts = [(sum(sizes[:k]), sizes[k]) for k in range(3)]

    def scratch(self):
        bufs = [
            pltpu.VMEM((SLOTS, 2, 2, 2, 2, self.rows, self.cols), F32),
            pltpu.VMEM((2, 2, 2, 2, self.rows, self.cols), F32),
        ]
        for _, size in self.parts:
            block = (size, self.cols) if self.by_rows else (self.rows, size)
            bufs += [pltpu.VMEM((2,) + (2,) * (2 - level) + block, F32) for level in range(3)]
        return bufs + [pltpu.SemaphoreType.DMA((2, 10)), pltpu.SemaphoreType.DMA((2, 10))]

    N_SCRATCH = 13

    def bind(self, refs, place):
        self.part, self.recv0 = refs[0], refs[1]
        self.land = [refs[2 + 3 * k : 5 + 3 * k] for k in range(3)]
        self.send_sem, self.recv_sem = refs[11], refs[12]
        self.core, self.coord, self.partner, self.neighbour = place

    def put(self, chunk, value):
        self.part[lax.rem(chunk, SLOTS)] = value.reshape(2, 2, 2, 2, self.rows, self.cols)

    def core_copy(self, chunk):
        par = lax.rem(chunk, 2)
        return pltpu.make_async_remote_copy(
            self.part.at[lax.rem(chunk, SLOTS), :, :, :, 1 - self.core], self.recv0.at[par],
            self.send_sem.at[par, 9], self.recv_sem.at[par, 9], device_id=self.partner, device_id_type=MESH,
        )

    def where(self, chunk, colour, level, other):
        order = COLOUR_AXES[colour]
        index = [slice(None)] * 3
        for pos in range(level + 1):
            axis = order[pos]
            index[axis] = 1 - self.coord[axis] if (other and pos == level) else self.coord[axis]
        start, size = self.parts[colour]
        tail = (pl.ds(start, size), slice(None)) if self.by_rows else (slice(None), pl.ds(start, size))
        return (lax.rem(chunk, SLOTS),) + tuple(index) + (self.core,) + tail

    def chip_copy(self, chunk, colour, level):
        slot, par = 3 * colour + level, lax.rem(chunk, 2)
        return pltpu.make_async_remote_copy(
            self.part.at[self.where(chunk, colour, level, True)], self.land[colour][level].at[par],
            self.send_sem.at[par, slot], self.recv_sem.at[par, slot],
            device_id=self.neighbour[COLOUR_AXES[colour][level]], device_id_type=MESH,
        )

    def send(self, chunk, stage):
        if stage == 0:
            self.core_copy(chunk).start()
        else:
            for colour in range(3):
                self.chip_copy(chunk, colour, stage - 1).start()

    def add(self, chunk, stage):
        slot, par = lax.rem(chunk, SLOTS), lax.rem(chunk, 2)
        if stage == 0:
            self.core_copy(chunk).wait()
            for z in range(2):
                for y in range(2):
                    self.part[slot, z, y, :, self.core] = self.part[slot, z, y, :, self.core] + self.recv0[par, z, y]
        else:
            for colour in range(3):
                self.chip_copy(chunk, colour, stage - 1).wait()
                mine = self.where(chunk, colour, stage - 1, False)
                self.part[mine] = self.part[mine] + self.land[colour][stage - 1][par]

    def result(self, chunk):
        return self.part[(lax.rem(chunk, SLOTS),) + tuple(self.coord) + (self.core,)] * (1.0 / 16.0)


def whole(shape):
    return pl.BlockSpec(shape, lambda i: (0,) * len(shape), pipeline_mode=pl.Buffered(1))


def row_block(tile, cols):
    return pl.BlockSpec((tile, cols), lambda i: (i, 0))


def shape_of(shape, dtype):
    return jax.ShapeDtypeStruct(shape, dtype)


def cost(flops):
    return pl.CostEstimate(flops=flops, bytes_accessed=60000000, transcendentals=0)


def forward(x_one, x_two, g_one, g_two, w_one, w_two):
    half, d = x_one.shape
    f = w_one.shape[1]
    rows, tile = 2 * half, 256
    switch = half // tile

    def kernel(x1, x2, g1, g2, w1, w2, xc, gc, p1, h2, act):
        step = pl.program_id(0)

        @pl.when(step < switch)
        def _():
            xc[...] = x1[...]
            gc[...] = g1[...]

        @pl.when(step >= switch)
        def _():
            xc[...] = x2[...]
            gc[...] = g2[...]

        for j in range(f // CHUNK):
            cs = pl.ds(j * CHUNK, CHUNK)
            pre = dot_nn(xc[...], w1[:, cs]).astype(BF16)
            p1[:, cs] = pre
            act[:, cs] = gelu_value(pre).astype(BF16)
        h2[...] = (dot_nn(act[...], w2[...]) + xc[...].astype(F32)).astype(BF16)

    first = pl.BlockSpec((tile, d), lambda i: (jnp.minimum(i, switch - 1), 0))
    second = pl.BlockSpec((tile, d), lambda i: (jnp.maximum(i - switch, 0), 0))
    narrow = shape_of((rows, d), BF16)
    return pl.pallas_call(
        kernel,
        name="forward",
        grid=(rows // tile,),
        in_specs=[first, second, first, second, whole((d, f)), whole((f, d))],
        out_specs=[row_block(tile, d), row_block(tile, d), row_block(tile, f), row_block(tile, d)],
        out_shape=[narrow, narrow, shape_of((rows, f), BF16), narrow],
        scratch_shapes=[pltpu.VMEM((tile, f), BF16)],
        cost_estimate=cost(4 * rows * d * f),
        compiler_params=pltpu.CompilerParams(vmem_limit_bytes=VMEM_LIMIT),
    )(x_one, x_two, g_one, g_two, w_one, w_two)


def column_grads(act, grad, w_up, pre, w_down, low, count, ident):
    rows, d = act.shape
    tall = Reducer(CHUNK // 16, d, False, 2)
    wide = Reducer(d // 16, CHUNK, True, 0)
    tile = 512

    def kernel(act_ref, grad_ref, src_ref, down_ref, dz_ref, tall_ref, wide_ref, hid, *refs):
        step = pl.program_id(0)
        dx_pos = lax.axis_index("dx")
        core = lax.rem(dx_pos, 2)
        coord = [lax.axis_index("dz"), lax.axis_index("dy"), dx_pos // 2]
        partner = {"dx": dx_pos + 1 - 2 * core}
        neighbour = [{"dz": 1 - coord[0]}, {"dy": 1 - coord[1]}, {"dx": lax.rem(dx_pos + 2, 4)}]
        place = (core, coord, partner, neighbour)
        tall.bind(refs[: Reducer.N_SCRATCH], place)
        wide.bind(refs[Reducer.N_SCRATCH :], place)
        barrier = pltpu.get_barrier_semaphore()

        @pl.when(step == 0)
        def _():
            for other in [partner] + neighbour:
                pl.semaphore_signal(barrier, inc=1, device_id=other, device_id_type=MESH)

        @pl.when(step < count)
        def _():
            for r in range(rows // tile):
                rs = pl.ds(r * tile, tile)
                if pre is None:
                    val = dot_nn(act_ref[rs, :], src_ref[...]).astype(BF16).astype(F32)
                else:
                    val = src_ref[rs, :].astype(F32)
                tanh_val = jnp.tanh(GELU_C * (val + GELU_A * val * val * val))
                hid[rs, :] = (0.5 * val * (1.0 + tanh_val)).astype(BF16)
                slope = 0.5 * (1.0 + tanh_val) + 0.5 * val * (1.0 - tanh_val * tanh_val) * GELU_C * (1.0 + 3.0 * GELU_A * val * val)
                dz_ref[rs, :] = (dot_nt(grad_ref[rs, :], down_ref[...]) * slope).astype(BF16)
            tall.put(step, dot_tn(hid[...], grad_ref[...]))
            wide.put(step, dot_tn(act_ref[...], dz_ref[...]))

        @pl.when(step == 0)
        def _():
            pl.semaphore_wait(barrier, 4)

        for stage in (3, 2, 1, 0):
            chunk = step - 1 - stage

            @pl.when(jnp.logical_and(chunk >= 0, chunk < count))
            def _():
                for red in (tall, wide):
                    red.add(chunk, stage)

        for stage in (3, 2, 1, 0):
            chunk = step - stage

            @pl.when(jnp.logical_and(chunk >= 0, chunk < count))
            def _():
                for red in (tall, wide):
                    red.send(chunk, stage)

        @pl.when(step >= 4)
        def _():
            tall_ref[0] = tall.result(step - 4)
            wide_ref[...] = wide.result(step - 4)

    last = count - 1
    up_spec = (
        pl.BlockSpec((d, CHUNK), lambda i: (0, low + jnp.minimum(i, last)))
        if pre is None
        else pl.BlockSpec((rows, CHUNK), lambda i: (0, low + jnp.minimum(i, last)))
    )
    return pl.pallas_call(
        kernel,
        grid=(count + 4,),
        in_specs=[
            whole((rows, d)), whole((rows, d)), up_spec,
            pl.BlockSpec((CHUNK, d), lambda i: (low + jnp.minimum(i, last), 0)),
        ],
        out_specs=[
            pl.BlockSpec((rows, CHUNK), lambda i: (0, jnp.minimum(i, last))),
            pl.BlockSpec((1, CHUNK // 16, d), lambda i: (jnp.maximum(i - 4, 0), 0, 0)),
            pl.BlockSpec((d // 16, CHUNK), lambda i: (0, jnp.maximum(i - 4, 0))),
        ],
        out_shape=[
            shape_of((rows, count * CHUNK), BF16),
            shape_of((count, CHUNK // 16, d), F32),
            shape_of((d // 16, count * CHUNK), F32),
        ],
        scratch_shapes=[pltpu.VMEM((rows, CHUNK), BF16)] + tall.scratch() + wide.scratch(),
        cost_estimate=cost((8 if pre is None else 6) * rows * d * CHUNK * count),
        compiler_params=pltpu.CompilerParams(vmem_limit_bytes=VMEM_LIMIT, collective_id=ident, has_side_effects=True),
    )(act, grad, w_up if pre is None else pre, w_down)


def skip_grad(grads, weight, skip, split):
    rows, d = skip.shape
    f = weight.shape[1]
    tile = 512
    half = rows // tile // 2
    widths = [part.shape[1] for part in grads]
    starts = [sum(widths[:k]) for k in range(len(widths))]

    def kernel(*refs):
        step = pl.program_id(0)
        parts, w, s, outs = refs[: len(grads)], refs[len(grads)], refs[len(grads) + 1], refs[len(grads) + 2 :]
        val = s[...].astype(F32)
        for part, start, width in zip(parts, starts, widths):
            val = val + dot_nt(part[...], w[:, start : start + width])
        val = val.astype(BF16)
        if not split:
            outs[0][...] = val
            return

        @pl.when(step < half)
        def _():
            outs[0][...] = val

        @pl.when(step >= half)
        def _():
            outs[1][...] = val

    if split:
        shapes = [shape_of((rows // 2, d), BF16)] * 2
        specs = [pl.BlockSpec((tile, d), lambda i: (jnp.minimum(i, half - 1), 0)),
                 pl.BlockSpec((tile, d), lambda i: (jnp.maximum(i - half, 0), 0))]
    else:
        shapes, specs = [shape_of((rows, d), BF16)], [row_block(tile, d)]
    return pl.pallas_call(
        kernel,
        grid=(rows // tile,),
        in_specs=[row_block(tile, width) for width in widths] + [whole((d, f)), row_block(tile, d)],
        out_specs=specs,
        out_shape=shapes,
        cost_estimate=cost(2 * rows * d * f),
        compiler_params=pltpu.CompilerParams(vmem_limit_bytes=VMEM_LIMIT),
    )(*grads, weight, skip)


def solution(mesh):
    row_spec = P(AXES, None)
    rep_spec = P(None, None)

    def gather(shard):
        return lax.all_gather(shard, AXES, axis=0, tiled=True)

    def pair_grads(act, grad, w_up, pre, w_down, cuts, ident):
        d = act.shape[1]
        dz, talls, wides = [], [], []
        for k, (low, high) in enumerate(zip(cuts[:-1], cuts[1:])):
            part, tall, wide = column_grads(act, grad, w_up, pre, w_down, low, high - low, ident + k)
            act, *_ = lax.optimization_barrier((act, tall, wide))
            dz.append(part)
            gathered_tall = gather(tall)
            wides.append(gather(wide))
            tall = gathered_tall.reshape(16, high - low, CHUNK // 16, d)
            talls.append(tall.transpose(1, 0, 2, 3).reshape((high - low) * CHUNK, d))
        return dz, talls, wides

    def step(x_one, g_one, x_two, g_two, w_one, w_two, w_three, w_four):
        xc, gc, p1, h2 = forward(x_one, x_two, g_one, g_two, w_one, w_two)
        dz3, four, three = pair_grads(h2, gc, w_three, None, w_four, CUTS_UPPER, 1)
        (dh2,) = skip_grad(dz3, w_three, gc, False)
        dz1, two, one = pair_grads(xc, dh2, None, p1, w_two, CUTS_LOWER, 4)
        dx_one, dx_two = skip_grad(dz1, w_one, dh2, True)
        dw_four, dw_two = jnp.concatenate(four, axis=0), jnp.concatenate(two, axis=0)
        dw_three, dw_one = jnp.concatenate(three, axis=1), jnp.concatenate(one, axis=1)
        return dw_one, dw_two, dw_three, dw_four, dx_one, dx_two

    return jax.shard_map(
        step,
        mesh=mesh,
        in_specs=(row_spec, row_spec, row_spec, row_spec, rep_spec, rep_spec, rep_spec, rep_spec),
        out_specs=(rep_spec, rep_spec, rep_spec, rep_spec, row_spec, row_spec),
        check_vma=False,
    )
```

time: 1460 us -> 731 us (0.50)
  waiting for transfers between devices: 917 us -> 213 us
  matrix products: 466 us -> 0 us
  Pallas kernels: 0 us -> 446 us
    dot_general x22 -> x0, matrix products: 466 us -> none  [the longest x8 189 us: mat_nt(): lax.dot_general(left_op, right_op, (((1,), (1,)), ((), ())), preferred_el...]
    pallas_call x0 -> x6, Pallas kernels: none -> 446 us  [the longest x3 320 us: column_grads(): pl.pallas_call(kernel, grid=(count + 4,), in_specs=[whole((rows, d)), who...]
    reduce_scatter x12 -> x0, waiting for transfers between devices: 382 us -> none  [the longest x4 160 us: mean_over_devices(): lax.psum_scatter(shard_sum, 'dy', scatter_dimension=0, tiled=True)]
    all_gather x12 -> x6, waiting for transfers between devices: 534 us -> 210 us  [gather(): return lax.all_gather(shard, AXES, axis=0, tiled=True)]
    unnamed x49 -> x1, local copies, waits for them, and re-layouts: 46.3 us -> 9.45 us
    transpose x0 -> x3, local copies, waits for them, and re-layouts: none -> 23.5 us  [pair_grads(): talls.append(tall.transpose(1, 0, 2, 3).reshape((high - low) * CHUNK, d))]
    concatenate x0 -> x2, other arithmetic: none -> 21.2 us  [the longest x1 11.5 us: step(): jnp.concatenate(two, axis=0)]
  transfers between devices with their start and end apart: 24 -> 6, of which waited for: 22 -> 6; matrix products, arithmetic and copies ran while one was open for 22% -> 6% of each run, Pallas kernels for 0% -> 4%
where the time goes in v1:
time: 731 us; the launch traced here: 728 us
  Pallas kernels  446 us (61%)
  waiting for transfers between devices  213 us (29%)
  local copies, waits for them, and re-layouts  32.9 us (5%)
  other arithmetic  21.2 us (3%)
  between operations  14.4 us (2%)
    pallas_call x3, Pallas kernels, column_grads(): pl.pallas_call(kernel, grid=(count + 4,), in_specs=[whole((rows, d)), who...  320 us
    all_gather x6, waiting for transfers between devices, gather(): return lax.all_gather(shard, AXES, axis=0, tiled=True)  210 us
    pallas_call x2, Pallas kernels, skip_grad(): pl.pallas_call(kernel, grid=(rows // tile,), in_specs=[row_block(tile, wi...  64.4 us
    pallas_call x1, Pallas kernels, forward(): pl.pallas_call(kernel, name='forward', grid=(rows // tile,), in_specs=[fi...  61.6 us
    transpose x3, local copies, waits for them, and re-layouts, pair_grads(): talls.append(tall.transpose(1, 0, 2, 3).reshape((high - low) * CHUNK, d))  23.5 us
  transfers between devices with their start and end apart: 6, of which 6 were waited for; matrix products, arithmetic and copies ran while one was open for 6% of the time, Pallas kernels for 4%

profile of v1, /device:TPU:0, one launch (start us, length us, event | category | flops | bytes accessed | tf_op | source)
XLA Modules:
  0.0 728.0 jit_solution(13729484188442035147)
XLA Ops:
  7.2 0.0 all-gather.13.cloned.1.call-start
  7.2 61.6 %forward.1 = (bf16[4096,1024]{1,0:T(8,128)(2,1)}, bf16[4096,1024]{1,0:T(8,128)(2,1)}, bf16[4096,2816]{1,0:T(8,128)(2,1)}, bf16[4096,1024]{1,0:T(8,128)(2,1)}) custom-call(bf16[2048,1024]{1,0:T(8,128)(2,1)} %x1.1, bf16[2048,1024]{1,0:T(8,128)(2,1)} %x2.1, bf16[2048,1024]{1,0:T(8,128)(2,1)} %g1.1, bf16[2048,1024]{1,0:T(8,128)(2,1)} %g2.1, ...), custom_call_target="tpu_custom_call" | custom-call | flops 47244640256 | bytes 60000000 | tf_op jit(solution)/shard_map/forward/pallas_call | solution.py:165
  68.8 162.4 %shard_map.127 = (bf16[4096,2816]{1,0:T(8,128)(2,1)}, f32[11,16,1024]{2,1,0:T(8,128)}, f32[64,2816]{1,0:T(8,128)}) custom-call(bf16[4096,1024]{1,0:T(8,128)(2,1)} %get-tuple-element.23.act_ref, bf16[4096,1024]{1,0:T(8,128)(2,1)} %get-tuple-element.24.grad_ref.refs_2_, bf16[1024,2816]{1,0:T(8,128)(2,1)} %refs_1_.1, bf16[2816,1024]{1,0:T(8,128)(2,1)} %down_ref.3), custom_call_target="tpu_custom_call" | custom-call | flops 94489280512 | bytes 60000000 | tf_op jit(solution)/shard_map/pallas_call | solution.py:247
  231.2 31.7 %shard_map.128.grad_ref.refs_3_ = bf16[4096,1024]{1,0:T(8,128)(2,1)} custom-call(bf16[4096,2816]{1,0:T(8,128)(2,1)} %get-tuple-element.25.refs_0_, bf16[1024,2816]{1,0:T(8,128)(2,1)} %refs_1_.1, bf16[4096,1024]{1,0:T(8,128)(2,1)} %get-tuple-element.24.grad_ref.refs_2_), custom_call_target="tpu_custom_call" | custom-call | flops 23622320128 | bytes 60000000 | tf_op jit(solution)/shard_map/pallas_call | solution.py:303
  262.9 83.5 %shard_map.129 = (bf16[4096,1536]{1,0:T(8,128)(2,1)}, f32[6,16,1024]{2,1,0:T(8,128)}, f32[64,1536]{1,0:T(8,128)}) custom-call(bf16[4096,1024]{1,0:T(8,128)(2,1)} %get-tuple-element.29.act_ref, bf16[4096,1024]{1,0:T(8,128)(2,1)} %shard_map.128.grad_ref.refs_3_, bf16[4096,2816]{1,0:T(8,128)(2,1)} %get-tuple-element.26.src_ref, bf16[2816,1024]{1,0:T(8,128)(2,1)} %down_ref.5), custom_call_target="tpu_custom_call" | custom-call | flops 38654705664 | bytes 60000000 | tf_op jit(solution)/shard_map/pallas_call | solution.py:247
  346.4 74.1 %shard_map.130 = (bf16[4096,1280]{1,0:T(8,128)(2,1)}, f32[5,16,1024]{2,1,0:T(8,128)}, f32[64,1280]{1,0:T(8,128)}) custom-call(bf16[4096,1024]{1,0:T(8,128)(2,1)} %get-tuple-element.29.act_ref, bf16[4096,1024]{1,0:T(8,128)(2,1)} %shard_map.128.grad_ref.refs_3_, bf16[4096,2816]{1,0:T(8,128)(2,1)} %get-tuple-element.26.src_ref, bf16[2816,1024]{1,0:T(8,128)(2,1)} %down_ref.5), custom_call_target="tpu_custom_call" | custom-call | flops 32212254720 | bytes 60000000 | tf_op jit(solution)/shard_map/pallas_call | solution.py:247
  420.6 0.0 all-gather.13.cloned.1.call-update
  420.6 0.0 all-gather.11.cloned.1.call-start
  420.6 0.7 all-gather.11.cloned.1.call-update
  421.3 0.0 all-gather.9.cloned.1.call-start
  421.4 0.7 all-gather.9.cloned.1.call-update
  422.1 0.0 all-gather.7.cloned.1.call-start
  422.1 0.5 all-gather.7.cloned.1.call-update
  422.7 0.0 all-gather.17.cloned.1.call-start
  422.7 0.5 all-gather.17.cloned.1.call-update
  423.2 0.0 all-gather.15.cloned.1.call-start
  423.3 0.5 all-gather.15.cloned.1.call-update
  423.8 32.7 %shard_map.131 = (bf16[2048,1024]{1,0:T(8,128)(2,1)}, bf16[2048,1024]{1,0:T(8,128)(2,1)}) custom-call(bf16[4096,1536]{1,0:T(8,128)(2,1)} %get-tuple-element.34.refs_0_, bf16[4096,1280]{1,0:T(8,128)(2,1)} %get-tuple-element.35.refs_1_, bf16[1024,2816]{1,0:T(8,128)(2,1)} %refs_2_.1, bf16[4096,1024]{1,0:T(8,128)(2,1)} %shard_map.128.grad_ref.refs_3_), custom_call_target="tpu_custom_call" | custom-call | flops 23622320128 | bytes 60000000 | tf_op jit(solution)/shard_map/pallas_call | solution.py:303
  456.5 2.6 all-gather.13.cloned.1.call-done
  459.0 5.7 copy.18
  464.7 38.7 %all-gather.11.cloned.1.call-done = f32[96,16,1024]{2,1,0:T(8,128)} async-done(((f32[6,16,1024]{2,1,0:T(8,128)}), f32[96,16,1024]{2,1,0:T(8,128)}) %all-gather.11.cloned.1.call-update) | async-done | bytes 6291472 | tf_op jit(solution)/shard_map/all_gather | solution.py:319
  503.4 6.6 copy.17
  510.0 11.5 %pad_maximum_fusion.1 = f32[2816,1024]{1,0:T(8,128)} fusion(f32[1280,1024]{1,0:T(8,128)} %bitcast.13, f32[1536,1024]{1,0:T(8,128)} %bitcast.12), kind=kLoop, calls=%fused_computation.1 | loop fusion | flops 2883584 | bytes 23068672 | tf_op jit(solution)/shard_map/concatenate | solution.py:340
  521.6 22.9 %all-gather.9.cloned.1.call-done = f32[1024,1280]{1,0:T(8,128)} async-done(((f32[64,1280]{1,0:T(8,128)}), f32[1024,1280]{1,0:T(8,128)}) %all-gather.9.cloned.1.call-update) | async-done | bytes 5242896 | tf_op jit(solution)/shard_map/all_gather | solution.py:319
  544.5 44.3 %all-gather.7.cloned.1.call-done = f32[1024,1536]{1,0:T(8,128)} async-done(((f32[64,1536]{1,0:T(8,128)}), f32[1024,1536]{1,0:T(8,128)}) %all-gather.7.cloned.1.call-update) | async-done | bytes 6291472 | tf_op jit(solution)/shard_map/all_gather | solution.py:319
  588.7 9.7 %pad_maximum_fusion = f32[1024,2816]{1,0:T(8,128)} fusion(f32[1024,1280]{1,0:T(8,128)} %all-gather.9.cloned.1.call-done, f32[1024,1536]{1,0:T(8,128)} %all-gather.7.cloned.1.call-done), kind=kLoop, calls=%fused_computation | loop fusion | flops 2883584 | bytes 23068672 | tf_op jit(solution)/shard_map/concatenate | solution.py:341
  598.4 51.7 %all-gather.17.cloned.1.call-done = f32[176,16,1024]{2,1,0:T(8,128)} async-done(((f32[11,16,1024]{2,1,0:T(8,128)}), f32[176,16,1024]{2,1,0:T(8,128)}) %all-gather.17.cloned.1.call-update) | async-done | bytes 11534352 | tf_op jit(solution)/shard_map/all_gather | solution.py:319
  650.1 11.2 %copy.19 = f32[11,16,16,1024]{3,2,1,0:T(8,128)} copy(f32[11,16,16,1024]{3,2,0,1:T(8,128)} %bitcast.14) | data formatting | bytes 23068672 | tf_op jit(solution)/shard_map/transpose | solution.py:331
  661.3 50.2 %all-gather.15.cloned.1.call-done = f32[1024,2816]{1,0:T(8,128)} async-done(((f32[64,2816]{1,0:T(8,128)}), f32[1024,2816]{1,0:T(8,128)}) %all-gather.15.cloned.1.call-update) | async-done | bytes 11534352 | tf_op jit(solution)/shard_map/all_gather | solution.py:319
  711.5 9.4 %copy.21 = f32[1024,2816]{1,0:T(8,128)} copy(f32[1024,2816]{1,0:T(8,128)} %all-gather.15.cloned.1.call-done) | data formatting | bytes 23068672
Async XLA Ops:
  7.2 451.9 %all-gather.13.cloned.1.call-start = ((), (), s32[]{:S(2)}) async-start(), calls=%async_computation.3 | async-start | bytes 5570560 | tf_op jit(solution)/shard_map/all_gather | solution.py:319
  420.6 82.8 %all-gather.11.cloned.1.call-start = ((), (), s32[]{:S(2)}) async-start(), calls=%async_computation.2 | async-start | bytes 6684672 | tf_op jit(solution)/shard_map/all_gather | solution.py:319
  421.3 123.1 %all-gather.9.cloned.1.call-start = ((), (), s32[]{:S(2)}) async-start(), calls=%async_computation.1 | async-start | bytes 5570560 | tf_op jit(solution)/shard_map/all_gather | solution.py:319
  422.1 166.6 %all-gather.7.cloned.1.call-start = ((), (), s32[]{:S(2)}) async-start(), calls=%async_computation | async-start | bytes 6684672 | tf_op jit(solution)/shard_map/all_gather | solution.py:319
  422.7 227.4 %all-gather.17.cloned.1.call-start = ((), (), s32[]{:S(2)}) async-start(), calls=%async_computation.5 | async-start | bytes 12255232 | tf_op jit(solution)/shard_map/all_gather | solution.py:319
  423.2 288.2 %all-gather.15.cloned.1.call-start = ((), (), s32[]{:S(2)}) async-start(), calls=%async_computation.4 | async-start | bytes 12255232 | tf_op jit(solution)/shard_map/all_gather | solution.py:319
Sparse Core Ops, SparseCore 0:
  420.7 38.2 all-gather.12
  461.3 42.1 all-gather.10
  505.7 38.7 all-gather.8
  546.5 42.1 all-gather.6
  590.8 59.2 all-gather.16
  652.2 59.2 all-gather.14

commit v2 on v1

v2 whole, which is shorter than its diff:
```python
import jax
import jax.numpy as jnp
from jax import lax
from jax.experimental import pallas as pl
from jax.experimental.pallas import tpu as pltpu
from jax.sharding import PartitionSpec as P

GELU_C = 0.7978845608028654
GELU_A = 0.044715
AXES = ("dz", "dy", "dx")
BF16 = jnp.bfloat16
F32 = jnp.float32
VMEM_LIMIT = 64000000
MESH = pl.DeviceIdType.MESH
CHUNK = 256
EARLY_UPPER = 5
EARLY_LOWER = 6
COLOUR_AXES = ((2, 1, 0), (1, 0, 2), (0, 2, 1))


def gelu_value(pre_act):
    pre_f = pre_act.astype(F32)
    return 0.5 * pre_f * (1.0 + jnp.tanh(GELU_C * (pre_f + GELU_A * pre_f * pre_f * pre_f)))


def gelu_both(val):
    square = val * val
    tanh_val = jnp.tanh(val * (GELU_C + (GELU_C * GELU_A) * square))
    half = 0.5 * val
    curve = half * (GELU_C + (3.0 * GELU_C * GELU_A) * square)
    return half + half * tanh_val, (0.5 + 0.5 * tanh_val) + curve * (1.0 - tanh_val * tanh_val)


def dot_nn(lhs, rhs):
    return lax.dot_general(lhs, rhs, (((1,), (0,)), ((), ())), preferred_element_type=F32)


def dot_nt(lhs, rhs):
    return lax.dot_general(lhs, rhs, (((1,), (1,)), ((), ())), preferred_element_type=F32)


def dot_tn(lhs, rhs):
    return lax.dot_general(lhs, rhs, (((0,), (0,)), ((), ())), preferred_element_type=F32)


class Reducer:
    def __init__(self, d, early):
        self.early = early
        self.slots = 10 if early else 5
        self.half = CHUNK // 16
        self.rows, self.cols = 2 * self.half, d
        tiles = d // 128
        sizes = [(tiles // 3 + (1 if k < tiles % 3 else 0)) * 128 for k in range(3)]
        self.parts = [(sum(sizes[:k]), sizes[k]) for k in range(3)]

    def scratch(self):
        bufs = [
            pltpu.VMEM((self.slots, 2, 2, 2, 2, self.rows, self.cols), F32),
            pltpu.VMEM((2, 2, 2, 2, self.rows, self.cols), F32),
        ]
        for _, size in self.parts:
            bufs += [pltpu.VMEM((2,) + (2,) * (2 - level) + (self.rows, size), F32) for level in range(3)]
        sems = [pltpu.SemaphoreType.DMA((2, 10)), pltpu.SemaphoreType.DMA((2, 10))]
        if self.early:
            sems += [pltpu.SemaphoreType.DMA((2, 10)), pltpu.SemaphoreType.DMA((2, 10)), pltpu.SemaphoreType.DMA((2,))]
        return bufs + sems

    def bind(self, refs, place):
        self.part, self.recv0 = refs[0], refs[1]
        self.land = [refs[2 + 3 * k : 5 + 3 * k] for k in range(3)]
        self.send_sem, self.recv_sem = refs[11], refs[12]
        if self.early:
            self.out_sem, self.in_sem, self.local_sem = refs[13:]
        self.core, self.coord, self.partner, self.neighbour = place

    def put_tall(self, chunk, value):
        shape = (2, 2, 2, 2, self.half, self.cols)
        self.part[lax.rem(chunk, self.slots), :, :, :, :, : self.half, :] = value.reshape(shape)

    def put_wide(self, chunk, value):
        pieces = value.reshape(2, 2, 2, 2, self.cols // CHUNK, self.half, CHUNK)
        for q in range(self.cols // CHUNK):
            where = (lax.rem(chunk, self.slots),) + (slice(None),) * 4 + (slice(self.half, None), slice(q * CHUNK, (q + 1) * CHUNK))
            self.part[where] = pieces[:, :, :, :, q]

    def core_copy(self, chunk):
        par = lax.rem(chunk, 2)
        return pltpu.make_async_remote_copy(
            self.part.at[lax.rem(chunk, self.slots), :, :, :, 1 - self.core], self.recv0.at[par],
            self.send_sem.at[par, 9], self.recv_sem.at[par, 9], device_id=self.partner, device_id_type=MESH,
        )

    def where(self, chunk, colour, level, other):
        order = COLOUR_AXES[colour]
        index = [slice(None)] * 3
        for pos in range(level + 1):
            axis = order[pos]
            index[axis] = 1 - self.coord[axis] if (other and pos == level) else self.coord[axis]
        start, size = self.parts[colour]
        return (lax.rem(chunk, self.slots),) + tuple(index) + (self.core, slice(None), pl.ds(start, size))

    def chip_copy(self, chunk, colour, level):
        slot, par = 3 * colour + level, lax.rem(chunk, 2)
        return pltpu.make_async_remote_copy(
            self.part.at[self.where(chunk, colour, level, True)], self.land[colour][level].at[par],
            self.send_sem.at[par, slot], self.recv_sem.at[par, slot],
            device_id=self.neighbour[COLOUR_AXES[colour][level]], device_id_type=MESH,
        )

    def send(self, chunk, stage):
        if stage == 0:
            self.core_copy(chunk).start()
        else:
            for colour in range(3):
                self.chip_copy(chunk, colour, stage - 1).start()

    def add(self, chunk, stage):
        slot, par = lax.rem(chunk, self.slots), lax.rem(chunk, 2)
        if stage == 0:
            self.core_copy(chunk).wait()
            for z in range(2):
                for y in range(2):
                    self.part[slot, z, y, :, self.core] = self.part[slot, z, y, :, self.core] + self.recv0[par, z, y]
        else:
            for colour in range(3):
                self.chip_copy(chunk, colour, stage - 1).wait()
                mine = self.where(chunk, colour, stage - 1, False)
                self.part[mine] = self.part[mine] + self.land[colour][stage - 1][par]

    def shard(self, chunk):
        return (lax.rem(chunk, self.slots),) + tuple(self.coord) + (self.core,)

    def spread_copies(self, chunk, stage):
        par = lax.rem(chunk, 2)
        if stage == 3:
            here = self.part.at[lax.rem(chunk, self.slots), :, :, :, self.core]
            return [pltpu.make_async_remote_copy(
                here, here, self.out_sem.at[par, 9], self.in_sem.at[par, 9],
                device_id=self.partner, device_id_type=MESH,
            )]
        level = 2 - stage
        copies = []
        for colour in range(3):
            here = self.part.at[self.where(chunk, colour, level, False)]
            slot = 3 * colour + level
            copies.append(pltpu.make_async_remote_copy(
                here, here, self.out_sem.at[par, slot], self.in_sem.at[par, slot],
                device_id=self.neighbour[COLOUR_AXES[colour][level]], device_id_type=MESH,
            ))
        return copies

    def store_copy(self, chunk, full_ref):
        return pltpu.make_async_copy(
            self.part.at[lax.rem(chunk, self.slots)], full_ref.at[chunk], self.local_sem.at[lax.rem(chunk, 2)]
        )


def whole(shape):
    return pl.BlockSpec(shape, lambda i: (0,) * len(shape), pipeline_mode=pl.Buffered(1))


def row_block(tile, cols):
    return pl.BlockSpec((tile, cols), lambda i: (i, 0))


def shape_of(shape, dtype):
    return jax.ShapeDtypeStruct(shape, dtype)


def cost(flops):
    return pl.CostEstimate(flops=flops, bytes_accessed=60000000, transcendentals=0)


def forward(x_one, x_two, g_one, g_two, w_one, w_two):
    half, d = x_one.shape
    f = w_one.shape[1]
    rows, tile = 2 * half, 512
    switch = half // tile

    def kernel(x1, x2, g1, g2, w1, w2, xc, gc, p1, h2, act):
        step = pl.program_id(0)

        @pl.when(step < switch)
        def _():
            xc[...] = x1[...]
            gc[...] = g1[...]

        @pl.when(step >= switch)
        def _():
            xc[...] = x2[...]
            gc[...] = g2[...]

        for j in range(f // CHUNK):
            cs = pl.ds(j * CHUNK, CHUNK)
            pre = dot_nn(xc[...], w1[:, cs]).astype(BF16)
            p1[:, cs] = pre
            act[:, cs] = gelu_value(pre).astype(BF16)
        h2[...] = (dot_nn(act[...], w2[...]) + xc[...].astype(F32)).astype(BF16)

    first = pl.BlockSpec((tile, d), lambda i: (jnp.minimum(i, switch - 1), 0))
    second = pl.BlockSpec((tile, d), lambda i: (jnp.maximum(i - switch, 0), 0))
    narrow = shape_of((rows, d), BF16)
    return pl.pallas_call(
        kernel,
        name="forward",
        grid=(rows // tile,),
        in_specs=[first, second, first, second, whole((d, f)), whole((f, d))],
        out_specs=[row_block(tile, d), row_block(tile, d), row_block(tile, f), row_block(tile, d)],
        out_shape=[narrow, narrow, shape_of((rows, f), BF16), narrow],
        scratch_shapes=[pltpu.VMEM((tile, f), BF16)],
        cost_estimate=cost(4 * rows * d * f),
        compiler_params=pltpu.CompilerParams(vmem_limit_bytes=VMEM_LIMIT),
    )(x_one, x_two, g_one, g_two, w_one, w_two)


def column_grads(act, grad, w_up, pre, w_down, ident, early, shift):
    rows, d = act.shape
    f = w_down.shape[0]
    count = f // CHUNK
    red = Reducer(d, early)
    tile = 512

    def kernel(act_ref, grad_ref, src_ref, down_ref, dz_ref, shard_ref, *refs):
        if early:
            full_ref, refs = refs[0], refs[1:]
        hid, refs = refs[0], refs[1:]
        step = pl.program_id(0)
        dx_pos = lax.axis_index("dx")
        core = lax.rem(dx_pos, 2)
        coord = [lax.axis_index("dz"), lax.axis_index("dy"), dx_pos // 2]
        partner = {"dx": dx_pos + 1 - 2 * core}
        neighbour = [{"dz": 1 - coord[0]}, {"dy": 1 - coord[1]}, {"dx": lax.rem(dx_pos + 2, 4)}]
        place = (core, coord, partner, neighbour)
        red.bind(refs, place)
        barrier = pltpu.get_barrier_semaphore()

        @pl.when(step == 0)
        def _():
            for other in [partner] + neighbour:
                pl.semaphore_signal(barrier, inc=1, device_id=other, device_id_type=MESH)

        @pl.when(step < count)
        def _():
            for r in range(rows // tile):
                rs = pl.ds(r * tile, tile)
                if pre is None:
                    val = dot_nn(act_ref[rs, :], src_ref[...]).astype(BF16).astype(F32)
                else:
                    val = src_ref[rs, :].astype(F32)
                hid_val, slope = gelu_both(val)
                hid[rs, :] = hid_val.astype(BF16)
                dz_ref[rs, :] = (dot_nt(grad_ref[rs, :], down_ref[...]) * slope).astype(BF16)
            red.put_tall(step, dot_tn(hid[...], grad_ref[...]))
            red.put_wide(step, dot_tn(act_ref[...], dz_ref[...]))

        @pl.when(step == 0)
        def _():
            pl.semaphore_wait(barrier, 4)

        def at(chunk, limit):
            return pl.when(jnp.logical_and(chunk >= 0, chunk < limit))

        if early:
            for stage in (3, 2, 1, 0):
                @at(step - 6 - stage, early)
                def _():
                    for copy in red.spread_copies(step - 6 - stage, stage):
                        copy.wait()

        for stage in (3, 2, 1, 0):
            @at(step - 1 - stage, count)
            def _():
                red.add(step - 1 - stage, stage)

        @pl.when(step >= 4)
        def _():
            mine = red.shard(step - 4)
            final = red.part[mine] * (1.0 / 16.0)
            red.part[mine] = final
            shard_ref[0] = final

        if early:
            @at(step - 9, early)
            def _():
                red.store_copy(step - 9, full_ref).start()

        for stage in (3, 2, 1, 0):
            @at(step - stage, count)
            def _():
                red.send(step - stage, stage)

        if early:
            for stage in (3, 2, 1, 0):
                @at(step - 5 - stage, early)
                def _():
                    for copy in red.spread_copies(step - 5 - stage, stage):
                        copy.start()

            @at(step - 9, early)
            def _():
                red.store_copy(step - 9, full_ref).wait()

    last = count - 1

    def at_chunk(i):
        return lax.rem(jnp.minimum(i, last) + shift, count)

    up_spec = pl.BlockSpec((d if pre is None else rows, CHUNK), lambda i: (0, at_chunk(i)))
    return pl.pallas_call(
        kernel,
        grid=(count + 4,),
        in_specs=[
            whole((rows, d)), whole((rows, d)), up_spec,
            pl.BlockSpec((CHUNK, d), lambda i: (at_chunk(i), 0)),
        ],
        out_specs=[
            pl.BlockSpec((rows, CHUNK), lambda i: (0, at_chunk(i))),
            pl.BlockSpec((1, CHUNK // 8, d), lambda i: (jnp.maximum(i - 4 - early, 0), 0, 0)),
        ] + ([pl.BlockSpec(memory_space=pl.ANY)] if early else []),
        out_shape=[
            shape_of((rows, count * CHUNK), BF16),
            shape_of((count - early, CHUNK // 8, d), F32),
        ] + ([shape_of((early, 2, 2, 2, 2, CHUNK // 8, d), F32)] if early else []),
        scratch_shapes=[pltpu.VMEM((rows, CHUNK), BF16)] + red.scratch(),
        cost_estimate=cost((8 if pre is None else 6) * rows * d * CHUNK * count),
        compiler_params=pltpu.CompilerParams(vmem_limit_bytes=VMEM_LIMIT, collective_id=ident, has_side_effects=True),
    )(act, grad, w_up if pre is None else pre, w_down)


def skip_grad(grad, weight, skip, split, places=()):
    rows, d = skip.shape
    f = weight.shape[1]
    tile = 512
    half = rows // tile // 2
    steps = rows // tile
    if split:
        shapes = [shape_of((rows // 2, d), BF16)] * 2
        specs = [pl.BlockSpec((tile, d), lambda i: (jnp.minimum(i, half - 1), 0)),
                 pl.BlockSpec((tile, d), lambda i: (jnp.maximum(i - half, 0), 0))]
    else:
        shapes, specs = [shape_of((rows, d), BF16)], [row_block(tile, d)]
    arrays, in_specs, slots = [], [], []
    group = 16 // steps
    for parts, runs in places:
        more, more_specs, place_out, place_shapes = place_specs(parts, runs, f // CHUNK, d, group)
        slots.append((3 + len(arrays), len(more), len(shapes), runs))
        arrays, in_specs = arrays + more, in_specs + more_specs
        shapes, specs = shapes + place_shapes, specs + place_out
    n_in = 3 + len(arrays)

    def kernel(*refs):
        step = pl.program_id(0)
        z, w, s = refs[:3]
        outs = refs[n_in:]
        val = dot_nt(z[...], w[...]) + s[...].astype(F32)
        val = val.astype(BF16)
        for first, n_parts, out, runs in slots:
            for device in range(group):
                place_shards(refs[first : first + n_parts], runs, outs[out], outs[out + 1], device)
        if not split:
            outs[0][...] = val
            return

        @pl.when(step < half)
        def _():
            outs[0][...] = val

        @pl.when(step >= half)
        def _():
            outs[1][...] = val

    return pl.pallas_call(
        kernel,
        grid=(steps,),
        in_specs=[row_block(tile, f), whole((d, f)), row_block(tile, d)] + in_specs,
        out_specs=specs,
        out_shape=shapes,
        cost_estimate=cost(2 * rows * d * f),
        compiler_params=pltpu.CompilerParams(vmem_limit_bytes=VMEM_LIMIT),
    )(grad, weight, skip, *arrays)


def place_shards(refs, runs, tall, wide, device):
    half = CHUNK // 16
    pieces = tall.shape[3] // CHUNK
    base = device * pieces * half
    for ref, (low, high, by_chunk) in zip(refs, runs):
        for j in range(high - low):
            block = ref[j, device] if by_chunk else ref[device, j]
            tall[low + j, device] = block[:half]
            for q in range(pieces):
                cols = slice((low + j) * CHUNK, (low + j + 1) * CHUNK)
                wide[base + q * half : base + (q + 1) * half, cols] = block[half:, q * CHUNK : (q + 1) * CHUNK]


def place_specs(parts, runs, total, d, group, shown=None):
    half = CHUNK // 16
    arrays, in_specs = [], []
    for part, (low, high, by_chunk) in zip(parts, runs):
        if by_chunk:
            arrays.append(part.reshape(high - low, 16, 2 * half, d))
            in_specs.append(pl.BlockSpec((high - low, group, 2 * half, d), lambda i: (0, i, 0, 0)))
        else:
            arrays.append(part.reshape(16, high - low, 2 * half, d))
            in_specs.append(pl.BlockSpec((group, high - low, 2 * half, d), lambda i: (i, 0, 0, 0)))
    shown = shown or total
    out_specs = [
        pl.BlockSpec((shown, group, half, d), lambda i: (0, i, 0, 0)),
        pl.BlockSpec((group * d // 16, shown * CHUNK), lambda i: (i, 0)),
    ]
    shapes = [shape_of((total, 16, half, d), F32), shape_of((d, total * CHUNK), F32)]
    return arrays, in_specs, out_specs, shapes


def assemble(parts, runs, total, d, into):
    arrays, in_specs, out_specs, shapes = place_specs(parts, runs, total, d, 1, runs[-1][1])
    n_parts = len(arrays)

    def kernel(*refs):
        place_shards(refs[:n_parts], runs, refs[-2], refs[-1], 0)

    return pl.pallas_call(
        kernel,
        grid=(16,),
        in_specs=in_specs + [pl.BlockSpec(memory_space=pl.ANY)] * 2,
        out_specs=out_specs,
        out_shape=shapes,
        input_output_aliases={n_parts: 0, n_parts + 1: 1},
        cost_estimate=pl.CostEstimate(flops=2000000000, bytes_accessed=16 * total * CHUNK * d, transcendentals=0),
        compiler_params=pltpu.CompilerParams(vmem_limit_bytes=VMEM_LIMIT),
    )(*arrays, *into)


def solution(mesh):
    row_spec = P(AXES, None)
    rep_spec = P(None, None)

    def gather(shard):
        return lax.all_gather(shard, AXES, axis=0, tiled=True)

    def step(x_one, g_one, x_two, g_two, w_one, w_two, w_three, w_four):
        xc, gc, p1, h2 = forward(x_one, x_two, g_one, g_two, w_one, w_two)
        f, d = w_four.shape
        total = f // CHUNK
        dz3, shard, up_first = column_grads(h2, gc, w_three, None, w_four, 1, EARLY_UPPER, 0)
        up_rest = gather(shard)
        (dh2,) = skip_grad(dz3, w_three, gc, False)
        shift = total - EARLY_LOWER
        dz1, shard, low_first = column_grads(xc, dh2, None, p1, w_two, 2, EARLY_LOWER, shift)
        low_rest = gather(shard)
        dx_one, dx_two, four, dw_three, two, dw_one = skip_grad(
            dz1, w_one, dh2, True,
            (((up_first, up_rest), ((0, EARLY_UPPER, True), (EARLY_UPPER, total, False))), ((low_first,), ((shift, total, True),))),
        )
        two, dw_one = assemble((low_rest,), ((0, shift, False),), total, d, (two, dw_one))
        dw_four, dw_two = four.reshape(f, d), two.reshape(f, d)
        return dw_one, dw_two, dw_three, dw_four, dx_one, dx_two

    return jax.shard_map(
        step,
        mesh=mesh,
        in_specs=(row_spec, row_spec, row_spec, row_spec, rep_spec, rep_spec, rep_spec, rep_spec),
        out_specs=(rep_spec, rep_spec, rep_spec, rep_spec, row_spec, row_spec),
        check_vma=False,
    )
```

time: 731 us -> 519 us (0.71)
  waiting for transfers between devices: 213 us -> 4.06 us
  Pallas kernels: 446 us -> 500 us
  local copies, waits for them, and re-layouts: 32.9 us -> 0 us
  other arithmetic: 21.2 us -> 0 us
    all_gather x6 -> x2, waiting for transfers between devices: 210 us -> 4.03 us  [gather(): return lax.all_gather(shard, AXES, axis=0, tiled=True)]
    pallas_call x2 -> x3, Pallas kernels: 64.4 us -> 96.2 us  [the longest x2 83.1 us: skip_grad(): pl.pallas_call(kernel, grid=(steps,), in_specs=[row_block(tile, f), whole...]
    pallas_call x3 -> x2, Pallas kernels: 320 us -> 346 us  [column_grads(): pl.pallas_call(kernel, grid=(count + 4,), in_specs=[whole((rows, d)), who...]
    transpose x3 -> x0, local copies, waits for them, and re-layouts: 23.5 us -> none  [pair_grads(): talls.append(tall.transpose(1, 0, 2, 3).reshape((high - low) * CHUNK, d))]
    concatenate x2 -> x0, other arithmetic: 21.2 us -> none  [the longest x1 11.5 us: step(): jnp.concatenate(two, axis=0)]
    unnamed x1 -> x0, local copies, waits for them, and re-layouts: 9.45 us -> none
  transfers between devices with their start and end apart: 6 -> 2, of which waited for: 6 -> 1; matrix products, arithmetic and copies ran while one was open for 6% -> 0% of each run, Pallas kernels for 4% -> 48%
where the time goes in v2:
time: 519 us; the launch traced here: 518 us
  Pallas kernels  500 us (96%)
  between operations  14.1 us (3%)
    pallas_call x2, Pallas kernels, column_grads(): pl.pallas_call(kernel, grid=(count + 4,), in_specs=[whole((rows, d)), who...  346 us
    pallas_call x2, Pallas kernels, skip_grad(): pl.pallas_call(kernel, grid=(steps,), in_specs=[row_block(tile, f), whole...  83.1 us
    pallas_call x1, Pallas kernels, forward(): pl.pallas_call(kernel, name='forward', grid=(rows // tile,), in_specs=[fi...  58.1 us
    pallas_call x1, Pallas kernels, assemble(): pl.pallas_call(kernel, grid=(16,), in_specs=in_specs + [pl.BlockSpec(memo...  13.1 us
  transfers between devices with their start and end apart: 2, of which 1 were waited for; matrix products, arithmetic and copies ran while one was open for 0% of the time, Pallas kernels for 48%

profile of v2, /device:TPU:0, one launch (start us, length us, event | category | flops | bytes accessed | tf_op | source)
XLA Modules:
  0.0 518.4 jit_solution(4195704283532949005)
XLA Ops:
  7.2 0.0 all-gather.5.cloned.1.call-start
  7.2 58.1 %forward.1 = (bf16[4096,1024]{1,0:T(8,128)(2,1)}, bf16[4096,1024]{1,0:T(8,128)(2,1)}, bf16[4096,2816]{1,0:T(8,128)(2,1)}, bf16[4096,1024]{1,0:T(8,128)(2,1)}) custom-call(bf16[2048,1024]{1,0:T(8,128)(2,1)} %x1.1, bf16[2048,1024]{1,0:T(8,128)(2,1)} %x2.1, bf16[2048,1024]{1,0:T(8,128)(2,1)} %g1.1, bf16[2048,1024]{1,0:T(8,128)(2,1)} %g2.1, ...), custom_call_target="tpu_custom_call" | custom-call | flops 47244640256 | bytes 60000000 | tf_op jit(solution)/shard_map/forward/pallas_call | solution.py:203
  65.4 181.9 %shard_map.127 = (bf16[4096,2816]{1,0:T(8,128)(2,1)}, f32[6,32,1024]{2,1,0:T(8,128)}, f32[5,2,2,2,2,32,1024]{6,5,4,3,2,1,0:T(8,128)}) custom-call(bf16[4096,1024]{1,0:T(8,128)(2,1)} %get-tuple-element.25.act_ref, bf16[4096,1024]{1,0:T(8,128)(2,1)} %get-tuple-element.26.grad_ref.refs_2_, bf16[1024,2816]{1,0:T(8,128)(2,1)} %refs_1_.2, bf16[2816,1024]{1,0:T(8,128)(2,1)} %down_ref.2), custom_call_target="tpu_custom_call" | custom-call | flops 94489280512 | bytes 60000000 | tf_op jit(solution)/shard_map/pallas_call | solution.py:309
  247.3 0.0 all-gather.5.cloned.1.call-update
  247.3 0.0 all-gather.3.cloned.1.call-start
  247.4 31.6 %shard_map.128.grad_ref.refs_2_ = bf16[4096,1024]{1,0:T(8,128)(2,1)} custom-call(bf16[4096,2816]{1,0:T(8,128)(2,1)} %get-tuple-element.27.refs_0_, bf16[1024,2816]{1,0:T(8,128)(2,1)} %refs_1_.2, bf16[4096,1024]{1,0:T(8,128)(2,1)} %get-tuple-element.26.grad_ref.refs_2_), custom_call_target="tpu_custom_call" | custom-call | flops 23622320128 | bytes 60000000 | tf_op jit(solution)/shard_map/pallas_call | solution.py:372
  279.0 164.0 %shard_map.129 = (bf16[4096,2816]{1,0:T(8,128)(2,1)}, f32[5,32,1024]{2,1,0:T(8,128)}, f32[6,2,2,2,2,32,1024]{6,5,4,3,2,1,0:T(8,128)}) custom-call(bf16[4096,1024]{1,0:T(8,128)(2,1)} %get-tuple-element.24.act_ref, bf16[4096,1024]{1,0:T(8,128)(2,1)} %shard_map.128.grad_ref.refs_2_, bf16[4096,2816]{1,0:T(8,128)(2,1)} %get-tuple-element.28.src_ref, ...), custom_call_target="tpu_custom_call" | custom-call | flops 70866960384 | bytes 60000000 | tf_op jit(solution)/shard_map/pallas_call | solution.py:309
  443.0 0.0 all-gather.3.cloned.1.call-update
  443.0 0.0 all-gather.5.cloned.1.call-done
  443.0 51.4 %shard_map.130 = (bf16[2048,1024]{1,0:T(8,128)(2,1)}, bf16[2048,1024]{1,0:T(8,128)(2,1)}, f32[11,16,16,1024]{3,2,1,0:T(8,128)}, f32[1024,2816]{1,0:T(8,128)}, f3...) custom-call(bf16[4096,2816]{1,0:T(8,128)(2,1)} %get-tuple-element.30.refs_0_, bf16[1024,2816]{1,0:T(8,128)(2,1)} %refs_1_.3, ...), custom_call_target="tpu_custom_call" | custom-call | flops 23622320128 | bytes 60000000 | tf_op jit(solution)/shard_map/pallas_call | solution.py:372
  494.5 4.0 all-gather.3.cloned.1.call-done
  498.5 13.1 %shard_map.131 = (f32[11,16,16,1024]{3,2,1,0:T(8,128)}, f32[1024,2816]{1,0:T(8,128)}) custom-call(f32[16,5,32,1024]{3,2,1,0:T(8,128)} %bitcast.7, f32[11,16,16,1024]{3,2,1,0:T(8,128)} %get-tuple-element.34.refs_1_, f32[1024,2816]{1,0:T(8,128)} %get-tuple-element.35.refs_2_), custom_call_target="tpu_custom_call", output_to_operand_aliasing={{0}: (1, {}), {1}: (2, {})} | custom-call | flops 2000000000 | bytes 46137344 | tf_op jit(solution)/shard_map/pallas_call | solution.py:422
Async XLA Ops:
  7.2 435.9 %all-gather.5.cloned.1.call-start = ((), (), s32[]{:S(2)}) async-start(), calls=%async_computation.1 | async-start | bytes 13369344 | tf_op jit(solution)/shard_map/all_gather | solution.py:439
  247.3 251.2 %all-gather.3.cloned.1.call-start = ((), (), s32[]{:S(2)}) async-start(), calls=%async_computation | async-start | bytes 11141120 | tf_op jit(solution)/shard_map/all_gather | solution.py:439
Sparse Core Ops, SparseCore 0:
  247.4 64.7 all-gather.4
  443.1 55.3 all-gather.2

commit v3 on v2

--- a/solution.py
+++ b/solution.py
@@ -13,8 +13,8 @@
 VMEM_LIMIT = 64000000
 MESH = pl.DeviceIdType.MESH
 CHUNK = 256
-EARLY_UPPER = 5
-EARLY_LOWER = 6
+EARLY_UPPER = 3
+EARLY_LOWER = 5
 COLOUR_AXES = ((2, 1, 0), (1, 0, 2), (0, 2, 1))
 
 
@@ -241,12 +241,13 @@
 
         @pl.when(step < count)
         def _():
+            if pre is None:
+                for r in range(rows // tile):
+                    rs = pl.ds(r * tile, tile)
+                    hid[rs, :] = dot_nn(act_ref[rs, :], src_ref[...]).astype(BF16)
             for r in range(rows // tile):
                 rs = pl.ds(r * tile, tile)
-                if pre is None:
-                    val = dot_nn(act_ref[rs, :], src_ref[...]).astype(BF16).astype(F32)
-                else:
-                    val = src_ref[rs, :].astype(F32)
+                val = (hid if pre is None else src_ref)[rs, :].astype(F32)
                 hid_val, slope = gelu_both(val)
                 hid[rs, :] = hid_val.astype(BF16)
                 dz_ref[rs, :] = (dot_nt(grad_ref[rs, :], down_ref[...]) * slope).astype(BF16)

time: 519 us -> 513 us (0.988)
  Pallas kernels: 500 us -> 488 us
  waiting for transfers between devices: 4.06 us -> 10.8 us
    pallas_call x2, Pallas kernels: 346 us -> 332 us  [column_grads(): pl.pallas_call(kernel, grid=(count + 4,), in_specs=[whole((rows, d)), who...]
    all_gather x2, waiting for transfers between devices: 4.03 us -> 10.7 us  [gather(): return lax.all_gather(shard, AXES, axis=0, tiled=True)]
  transfers between devices with their start and end apart: 2 -> 2, of which waited for: 1 -> 1; matrix products, arithmetic and copies ran while one was open for 0% -> 0% of each run, Pallas kernels for 48% -> 49%
where the time goes in v3:
time: 513 us; the launch traced here: 512 us
  Pallas kernels  488 us (95%)
  between operations  14.1 us (3%)
  waiting for transfers between devices  10.8 us (2%)
    pallas_call x2, Pallas kernels, column_grads(): pl.pallas_call(kernel, grid=(count + 4,), in_specs=[whole((rows, d)), who...  332 us
    pallas_call x2, Pallas kernels, skip_grad(): pl.pallas_call(kernel, grid=(steps,), in_specs=[row_block(tile, f), whole...  82.8 us
    pallas_call x1, Pallas kernels, forward(): pl.pallas_call(kernel, name='forward', grid=(rows // tile,), in_specs=[fi...  58.1 us
    pallas_call x1, Pallas kernels, assemble(): pl.pallas_call(kernel, grid=(16,), in_specs=in_specs + [pl.BlockSpec(memo...  15.1 us
    all_gather x2, waiting for transfers between devices, gather(): return lax.all_gather(shard, AXES, axis=0, tiled=True)  10.7 us
  transfers between devices with their start and end apart: 2, of which 1 were waited for; matrix products, arithmetic and copies ran while one was open for 0% of the time, Pallas kernels for 49%

profile of v3, /device:TPU:0, one launch (start us, length us, event | category | flops | bytes accessed | tf_op | source)
XLA Modules:
  0.0 512.5 jit_solution(2435985437899302802)
XLA Ops:
  7.2 0.0 all-gather.5.cloned.1.call-start
  7.2 58.1 %forward.1 = (bf16[4096,1024]{1,0:T(8,128)(2,1)}, bf16[4096,1024]{1,0:T(8,128)(2,1)}, bf16[4096,2816]{1,0:T(8,128)(2,1)}, bf16[4096,1024]{1,0:T(8,128)(2,1)}) custom-call(bf16[2048,1024]{1,0:T(8,128)(2,1)} %x1.1, bf16[2048,1024]{1,0:T(8,128)(2,1)} %x2.1, bf16[2048,1024]{1,0:T(8,128)(2,1)} %g1.1, bf16[2048,1024]{1,0:T(8,128)(2,1)} %g2.1, ...), custom_call_target="tpu_custom_call" | custom-call | flops 47244640256 | bytes 60000000 | tf_op jit(solution)/shard_map/forward/pallas_call | solution.py:203
  65.4 165.6 %shard_map.127 = (bf16[4096,2816]{1,0:T(8,128)(2,1)}, f32[8,32,1024]{2,1,0:T(8,128)}, f32[3,2,2,2,2,32,1024]{6,5,4,3,2,1,0:T(8,128)}) custom-call(bf16[4096,1024]{1,0:T(8,128)(2,1)} %get-tuple-element.25.act_ref, bf16[4096,1024]{1,0:T(8,128)(2,1)} %get-tuple-element.26.grad_ref.refs_2_, bf16[1024,2816]{1,0:T(8,128)(2,1)} %refs_1_.2, bf16[2816,1024]{1,0:T(8,128)(2,1)} %down_ref.2), custom_call_target="tpu_custom_call" | custom-call | flops 94489280512 | bytes 60000000 | tf_op jit(solution)/shard_map/pallas_call | solution.py:310
  231.0 0.0 all-gather.5.cloned.1.call-update
  231.0 0.0 all-gather.3.cloned.1.call-start
  231.0 31.6 %shard_map.128.grad_ref.refs_2_ = bf16[4096,1024]{1,0:T(8,128)(2,1)} custom-call(bf16[4096,2816]{1,0:T(8,128)(2,1)} %get-tuple-element.27.refs_0_, bf16[1024,2816]{1,0:T(8,128)(2,1)} %refs_1_.2, bf16[4096,1024]{1,0:T(8,128)(2,1)} %get-tuple-element.26.grad_ref.refs_2_), custom_call_target="tpu_custom_call" | custom-call | flops 23622320128 | bytes 60000000 | tf_op jit(solution)/shard_map/pallas_call | solution.py:373
  262.6 165.9 %shard_map.129 = (bf16[4096,2816]{1,0:T(8,128)(2,1)}, f32[6,32,1024]{2,1,0:T(8,128)}, f32[5,2,2,2,2,32,1024]{6,5,4,3,2,1,0:T(8,128)}) custom-call(bf16[4096,1024]{1,0:T(8,128)(2,1)} %get-tuple-element.24.act_ref, bf16[4096,1024]{1,0:T(8,128)(2,1)} %shard_map.128.grad_ref.refs_2_, bf16[4096,2816]{1,0:T(8,128)(2,1)} %get-tuple-element.28.src_ref, ...), custom_call_target="tpu_custom_call" | custom-call | flops 70866960384 | bytes 60000000 | tf_op jit(solution)/shard_map/pallas_call | solution.py:310
  428.6 0.0 all-gather.3.cloned.1.call-update
  428.6 0.0 all-gather.5.cloned.1.call-done
  428.6 51.2 %shard_map.130 = (bf16[2048,1024]{1,0:T(8,128)(2,1)}, bf16[2048,1024]{1,0:T(8,128)(2,1)}, f32[11,16,16,1024]{3,2,1,0:T(8,128)}, f32[1024,2816]{1,0:T(8,128)}, f3...) custom-call(bf16[4096,2816]{1,0:T(8,128)(2,1)} %get-tuple-element.30.refs_0_, bf16[1024,2816]{1,0:T(8,128)(2,1)} %refs_1_.3, ...), custom_call_target="tpu_custom_call" | custom-call | flops 23622320128 | bytes 60000000 | tf_op jit(solution)/shard_map/pallas_call | solution.py:373
  479.8 10.7 %all-gather.3.cloned.1.call-done = f32[96,32,1024]{2,1,0:T(8,128)} async-done(((f32[6,32,1024]{2,1,0:T(8,128)}), f32[96,32,1024]{2,1,0:T(8,128)}) %all-gather.3.cloned.1.call-update) | async-done | bytes 12582928 | tf_op jit(solution)/shard_map/all_gather | solution.py:440
  490.5 15.1 %shard_map.131 = (f32[11,16,16,1024]{3,2,1,0:T(8,128)}, f32[1024,2816]{1,0:T(8,128)}) custom-call(f32[16,6,32,1024]{3,2,1,0:T(8,128)} %bitcast.6, f32[11,16,16,1024]{3,2,1,0:T(8,128)} %get-tuple-element.34.refs_1_, f32[1024,2816]{1,0:T(8,128)} %get-tuple-element.35.refs_2_), custom_call_target="tpu_custom_call", output_to_operand_aliasing={{0}: (1, {}), {1}: (2, {})} | custom-call | flops 2000000000 | bytes 46137344 | tf_op jit(solution)/shard_map/pallas_call | solution.py:423
Async XLA Ops:
  7.2 421.5 %all-gather.5.cloned.1.call-start = ((), (), s32[]{:S(2)}) async-start(), calls=%async_computation.1 | async-start | bytes 17825792 | tf_op jit(solution)/shard_map/all_gather | solution.py:440
  231.0 259.5 %all-gather.3.cloned.1.call-start = ((), (), s32[]{:S(2)}) async-start(), calls=%async_computation | async-start | bytes 13369344 | tf_op jit(solution)/shard_map/all_gather | solution.py:440
Sparse Core Ops, SparseCore 0:
  231.1 90.4 all-gather.4
  428.7 61.7 all-gather.2
